TPU v7x, 32 devices: a whole 2x2x4 slice. The times are simulated.
32 devices in a mesh: facet: 8 (over z, x), col: 4 (over y, core).
Axes of the slice: x: 2, y: 2, z: 4, core: 2. Of those that a mesh axis runs over, the one named last changes fastest.
Arguments:
- facets: bfloat16 [2, 8192, 1024], P(None, ('facet', 'col')), may hold values from -6 to 6
- observed: float32 [2, 32, 1024], P(None, 'col'), may hold values from -6 to 6
- uv_cells: int32 [2, 32, 1024], P(None, 'col'), may hold values from 0 to 511
- counts: int32 [32], P('col'), may hold values from 64 to 1024, as said below
Outputs:
- facet_residual: float32 [2, 8192, 1024], P(None, ('facet', 'col'))
Inputs may be any that keep to these rules, and one draw needn't show every extreme that they name: Live slots of a subgrid are its first counts[s] slots; in every column some subgrid has all 1024 slots live.
All inputs are finite; a program needn't handle non-finite values.
Results may differ from a plain program's by a relative error of at most 0.008.
Values may be sent and summed in bfloat16 or wider, within the bound.
A program may use at most 64 MiB of HBM per device.

v0:
```python
import functools
import math

import jax
import jax.numpy as jnp
import numpy as np
from jax import lax
from jax.experimental import pallas as pl
from jax.experimental.pallas import tpu as pltpu
from jax.sharding import PartitionSpec as P

S = 512
IMAGE = 65536
MESH = pl.DeviceIdType.MESH
BF = jnp.bfloat16
F32 = jnp.float32


def unit(ticks):
    angle = (np.asarray(ticks, np.int64) % IMAGE) * (-2.0 * math.pi / IMAGE)
    return np.cos(angle), np.sin(angle)


def make_constants(facets, columns, per_column, extent):
    window = S // 8
    spacing = IMAGE // extent
    parts = window // 16
    cells = np.arange(extent, dtype=np.int64)
    weight = (0.6 + 0.4 * np.sin(math.pi * (cells + 0.5) / extent) ** 2) / math.sqrt(extent)
    low = np.arange(16, dtype=np.int64)
    high = 16 * np.arange(parts, dtype=np.int64)
    col = np.arange(columns, dtype=np.int64)
    vc = col * (IMAGE // 4) + (29 * col + 3) % spacing
    sub = np.arange(per_column, dtype=np.int64)
    us = sub * (IMAGE // 64) + (37 * sub + 5) % (IMAGE * 8 // S)
    grain = IMAGE // window
    rows = []
    for ticks, scale in (
        (spacing * low[:, None] * cells, 1.0),
        ((vc[:, None] + spacing * high).reshape(-1, 1) * cells, weight),
        (grain * low[:, None] * cells, 1.0),
        ((us[:, None] + grain * high).reshape(-1, 1) * cells, weight),
    ):
        real, imag = unit(ticks)
        rows += [real * scale, imag * scale]
    groups = max(facets // 8, 1)
    wide = max(columns, per_column)
    scalars = np.zeros((8 + groups, 2 * wide))
    for index in range(8):
        real, imag = unit(index * extent * vc)
        scalars[index, :columns] = real
        scalars[index, wide : wide + columns] = imag
    for index in range(groups):
        real, imag = unit(index * extent * us)
        scalars[8 + index, :per_column] = real
        scalars[8 + index, wide : wide + per_column] = imag
    return np.concatenate(rows).astype(np.float32), scalars.astype(np.float32)


def spin(value, first, second):
    half = value.shape[1] // 2
    lane = lax.broadcasted_iota(jnp.int32, value.shape, 1)
    return pltpu.roll(value, half, 1) * jnp.where(lane < half, first, second)


def cycle_kernel(
    nf, nc, x_hbm, obs_hbm, cells_hbm, counts, con_hbm, scal, back_out, tab,
    xbuf, obs, cells, con, t2, tt, s_send, s_recv, g_send, g_recv, lt, rtr, rti, r1r, r1i, wt,
    r_send, r_recv, b_send, b_recv,
    in_sem, sa, ra, sb, rb, sc, rc, sd, rd,
):
    f = lax.axis_index("facet")
    c = lax.axis_index("col")
    window = S // 8
    two = 2 * window
    parts = window // 16
    pc = nf
    rows = xbuf.shape[1]
    groups = nf // 8
    wide = max(nc, pc)
    vis = obs.shape[2]
    if nc % 2:
        col_steps = [(d, 0) for d in range(1, nc)]
    else:
        col_steps = [(d, k) for d in range(nc // 2 - 1, -1, -1) for k in range(2) if d or k]

    def col_at(step, sign):
        if nc % 2:
            return lax.rem(c + nc + sign * step[0], nc)
        top = lax.rem(c // 2 + nc // 2 + sign * step[0], nc // 2)
        return 2 * top + lax.rem(c + step[1], 2)

    def pair_at(q):
        return lax.rem(f // 2 + q, 4)

    def facet_link(src_buf, dst_buf, send, recv, peer, slot):
        return pltpu.make_async_remote_copy(
            src_buf.at[peer], dst_buf.at[slot], send.at[peer], recv.at[slot], (peer, c), MESH
        )

    def col_link(src_buf, dst_buf, send, recv, peer, slot):
        return pltpu.make_async_remote_copy(
            src_buf.at[peer], dst_buf.at[slot], send.at[peer], recv.at[slot], (f, peer), MESH
        )

    barrier = pltpu.get_barrier_semaphore()
    for d in range(1, nc):
        pl.semaphore_signal(barrier, inc=1, device_id=(f, lax.rem(c + d, nc)), device_id_type=MESH)
    for d in range(1, nf):
        pl.semaphore_signal(barrier, inc=1, device_id=(lax.rem(f + d, nf), c), device_id_type=MESH)

    e1 = 32
    f0 = e1 + 2 * nc * parts
    h0 = f0 + 32
    last = con.shape[0]
    loads = [
        pltpu.make_async_copy(con_hbm.at[0:f0], con.at[0:f0], in_sem.at[0]),
        pltpu.make_async_copy(x_hbm, xbuf, in_sem.at[1]),
        pltpu.make_async_copy(con_hbm.at[f0:last], con.at[f0:last], in_sem.at[2]),
        pltpu.make_async_copy(obs_hbm, obs, in_sem.at[3]),
        pltpu.make_async_copy(cells_hbm, cells, in_sem.at[4]),
    ]
    for load in loads:
        load.start()
    nt = (((1,), (1,)), ((), ()))
    fm = lax.rem(f, 8)

    def column_table(cp):
        pr, pi = scal[fm, cp], scal[fm, wide + cp]
        lr, lm = con[0:16, :], con[16:32, :]
        for li in range(parts):
            i = cp * parts + li
            ar, ai = con[pl.ds(e1 + i, 1), :], con[pl.ds(e1 + nc * parts + i, 1), :]
            er, ei = ar * pr - ai * pi, ar * pi + ai * pr
            real = (lr * er - lm * ei).astype(BF)
            imag = (lr * ei + lm * er).astype(BF)
            top = pl.multiple_of(cp * two + li * 16, 16)
            low = pl.multiple_of(cp * two + window + li * 16, 16)
            tab[0, pl.ds(top, 16), :] = real
            tab[0, pl.ds(low, 16), :] = imag
            tab[1, pl.ds(top, 16), :] = -imag
            tab[1, pl.ds(low, 16), :] = real

    def column_strip(cp):
        at = pl.multiple_of(cp * two, two)
        strip = lax.dot_general(xbuf[0], tab[0, pl.ds(at, two), :], nt, preferred_element_type=F32)
        strip += lax.dot_general(xbuf[1], tab[1, pl.ds(at, two), :], nt, preferred_element_type=F32)
        s_send[cp] = strip.astype(BF)

    loads[0].wait()
    for n, step in enumerate(col_steps):
        peer = col_at(step, 1)
        column_table(peer)
        if n == 0:
            loads[1].wait()
        column_strip(peer)
        if n == 0:
            pl.semaphore_wait(barrier, nc - 1 + nf - 1)
        col_link(s_send, s_recv, sa, ra, peer, c).start()
    column_table(c)
    column_strip(c)

    half = pc * window
    fg = f // 8

    loads[2].wait()

    def row_body(i, carry):
        j = i // parts
        ki = i - j * parts
        pr, pi = scal[8 + fg, j], scal[8 + fg, wide + j]
        ar, ai = con[pl.ds(h0 + i, 1), :], con[pl.ds(h0 + pc * parts + i, 1), :]
        er, ei = ar * pr - ai * pi, ar * pi + ai * pr
        lr, lm = con[f0 : f0 + 16, :], con[f0 + 16 : f0 + 32, :]
        at = pl.multiple_of(j * window + ki * 16, 16)
        t2[pl.ds(at, 16), :] = (lr * er - lm * ei).astype(BF)
        t2[pl.ds(pl.multiple_of(half + at, 16), 16), :] = (lr * ei + lm * er).astype(BF)
        return carry

    lax.fori_loop(0, pc * parts, row_body, 0)

    def part_product(src, block):
        start = pl.multiple_of(src * rows, rows)
        return jnp.dot(t2[:, pl.ds(start, rows)], block, preferred_element_type=F32)

    acc = part_product(c, s_send[c])
    for step in col_steps[::-1]:
        src = col_at(step, -1)
        col_link(s_send, s_recv, sa, ra, src, src).wait_recv()
        acc += part_product(src, s_recv[src])
    win = (acc[:half] + spin(acc[half:], -1.0, 1.0)).astype(BF)
    for j in range(pc):
        g_send[j] = win[j * window : (j + 1) * window]

    def each_facet(q, act):
        pair = pair_at(q)
        for g in range(groups):
            for h in range(2):
                index = g * 8 + 2 * pair + h
                if q == 0:
                    pl.when(index != f)(functools.partial(act, index))
                else:
                    act(index)

    def send_window(index):
        facet_link(g_send, g_recv, sb, rb, index, f).start()

    def take_window(index):
        facet_link(g_send, g_recv, sb, rb, index, index).wait_recv()

    def send_back(index):
        facet_link(r_send, r_recv, sc, rc, index, f).start()

    def take_back(index):
        facet_link(r_send, r_recv, sc, rc, index, index).wait_recv()

    far_first = (2, 3, 1, 0)
    for q in far_first:
        each_facet(q, send_window)
    g_recv[f] = g_send[f]

    loads[3].wait()
    loads[4].wait()
    first = cells[0, pl.ds(f, 1), :]
    second = cells[1, pl.ds(f, 1), :]

    def wave(count, step, cell):
        index = step * lax.broadcasted_iota(jnp.int32, (count, vis), 0)
        angle = (index * cell & (S - 1)).astype(F32) * (-2.0 * math.pi / S)
        return jnp.cos(angle), jnp.sin(angle)

    l0r, l0i = wave(16, 1, first)
    l1r, l1i = wave(max(groups * parts, 8), 16, first)
    for i in range(groups * parts):
        er, ei = l1r[i : i + 1], l1i[i : i + 1]
        g, k = i // parts, i % parts
        at = g * two + k * 16
        lt[at : at + 16, :] = (l0r * er - l0i * ei).astype(BF)
        lt[at + window : at + window + 16, :] = (l0r * ei + l0i * er).astype(BF)
    m0r, m0i = wave(16, 1, second)
    r1r[...], r1i[...] = wave(S // 16, 16, second)

    def right_body(i, carry):
        er, ei = r1r[pl.ds(i, 1), :], r1i[pl.ds(i, 1), :]
        at = pl.multiple_of(i * 16, 16)
        rtr[pl.ds(at, 16), :] = m0r * er - m0i * ei
        rti[pl.ds(at, 16), :] = m0r * ei + m0i * er
        return carry

    lax.fori_loop(0, S // 16, right_body, 0)

    pred_r = jnp.zeros((8, vis), F32)
    pred_i = jnp.zeros((8, vis), F32)
    for q in far_first[::-1]:
        each_facet(q, take_window)
        for h in range(2):
            b = 2 * pair_at(q) + h
            inner = None
            for g in range(groups):
                block = g_recv[g * 8 + b].astype(F32)
                both = jnp.concatenate([block, spin(block, -1.0, 1.0)], axis=0)
                term = jnp.dot(
                    both.T.astype(BF), lt[g * two : (g + 1) * two, :], preferred_element_type=F32
                )
                inner = term if inner is None else inner + term
            ir, ii = inner[:window], inner[window:]
            at = pl.multiple_of(b * window, window)
            rr, ri = rtr[pl.ds(at, window), :], rti[pl.ds(at, window), :]
            pred_r += jnp.sum((ir * rr - ii * ri).reshape(window // 8, 8, vis), axis=0)
            pred_i += jnp.sum((ir * ri + ii * rr).reshape(window // 8, 8, vis), axis=0)
    live = lax.broadcasted_iota(jnp.int32, (1, vis), 1) < counts[f]
    res_r = jnp.where(
        live, obs[0, pl.ds(f, 1), :] - jnp.sum(pred_r, axis=0, keepdims=True) / S, 0.0
    )
    res_i = jnp.where(
        live, obs[1, pl.ds(f, 1), :] - jnp.sum(pred_i, axis=0, keepdims=True) / S, 0.0
    )

    scale = 1.0 / math.sqrt(vis)
    for n, q in enumerate(far_first):
        base = n * 2 * two
        for h in range(2):
            at = pl.multiple_of((2 * pair_at(q) + h) * window, window)
            rr, ri = rtr[pl.ds(at, window), :], rti[pl.ds(at, window), :]
            low = base + h * two
            wt[low : low + window, :] = (res_r * rr + res_i * ri).astype(BF)
            wt[low + window : low + two, :] = (res_i * rr - res_r * ri).astype(BF)
        grid = lax.dot_general(
            lt[...], wt[base : base + 2 * two, :], nt, preferred_element_type=F32
        )
        for g in range(groups):
            for h in range(2):
                u = grid[g * two : g * two + window, h * two : (h + 1) * two]
                v = grid[g * two + window : (g + 1) * two, h * two : (h + 1) * two]
                index = g * 8 + 2 * pair_at(q) + h
                r_send[index] = ((u + spin(v, 1.0, -1.0)) * scale).astype(BF)
        each_facet(q, send_back)
    r_recv[f] = r_send[f]
    for i in range(2 * half // 256):
        tt[:, i * 256 : (i + 1) * 256] = t2[i * 256 : (i + 1) * 256, :].T
    for q in far_first[::-1]:
        each_facet(q, take_back)

    ret = r_recv[...].reshape(half, two)
    other = spin(ret.astype(F32), 1.0, -1.0).astype(BF)

    def back_strip(cp):
        at = pl.multiple_of(cp * rows, rows)
        strip = jnp.dot(tt[pl.ds(at, rows), :half], ret, preferred_element_type=F32)
        strip += jnp.dot(tt[pl.ds(at, rows), half:], other, preferred_element_type=F32)
        b_send[cp] = strip.astype(BF)

    for step in col_steps:
        peer = col_at(step, 1)
        back_strip(peer)
        col_link(b_send, b_recv, sd, rd, peer, c).start()
    back_strip(c)
    back_out[c] = b_send[c]
    for step in col_steps[::-1]:
        src = col_at(step, -1)
        col_link(b_send, b_recv, sd, rd, src, src).wait_recv()
        back_out[src] = b_recv[src]
    for step in col_steps:
        peer = col_at(step, 1)
        col_link(s_send, s_recv, sa, ra, peer, c).wait_send()
        col_link(b_send, b_recv, sd, rd, peer, c).wait_send()
    for d in range(1, nf):
        peer = lax.rem(f + d, nf)
        facet_link(g_send, g_recv, sb, rb, peer, f).wait_send()
        facet_link(r_send, r_recv, sc, rc, peer, f).wait_send()


def image_kernel(nc, back, tab, out, buf, sem):
    tiles, tile = buf.shape[0], buf.shape[3]
    strip = jnp.concatenate([back[k] for k in range(nc)], axis=1)
    stores = []
    for t in range(tiles):
        for part in range(2):
            piece = tab[part, :, t * tile : (t + 1) * tile]
            buf[t, part] = jnp.dot(strip, piece, preferred_element_type=F32)
        store = pltpu.make_async_copy(
            buf.at[t], out.at[:, :, t * tile : (t + 1) * tile], sem.at[t]
        )
        store.start()
        stores.append(store)
    for store in stores:
        store.wait()


def solution(mesh):
    nf, nc = mesh.shape["facet"], mesh.shape["col"]

    def on_device(facets, observed, uv_cells, counts):
        rows, extent = facets.shape[1:]
        vis = observed.shape[2]
        pc = counts.shape[0]
        window = S // 8
        two = 2 * window
        groups = nf // 8
        assert pc == nf and nf % 8 == 0 and nf <= 32
        con, scal = make_constants(nf, nc, pc, extent)
        vmem = pl.BlockSpec(memory_space=pltpu.VMEM)
        smem = pl.BlockSpec(memory_space=pltpu.SMEM)
        hbm = pl.BlockSpec(memory_space=pltpu.HBM)
        dma = pltpu.SemaphoreType.DMA
        fixed = functools.partial(pltpu.with_memory_space_constraint, memory_space=pltpu.HBM)
        back, tab = pl.pallas_call(
            functools.partial(cycle_kernel, nf, nc),
            out_shape=(
                jax.ShapeDtypeStruct((nc, rows, two), BF),
                jax.ShapeDtypeStruct((2, nc * two, extent), BF),
            ),
            in_specs=[hbm, hbm, hbm, smem, hbm, smem],
            out_specs=(vmem, vmem),
            scratch_shapes=[
                pltpu.VMEM((2, rows, extent), BF),
                pltpu.VMEM((2, pc, vis), F32),
                pltpu.VMEM((2, pc, vis), jnp.int32),
                pltpu.VMEM(con.shape, F32),
                pltpu.VMEM((2 * pc * window, extent), BF),
                pltpu.VMEM((extent, 2 * pc * window), BF),
                pltpu.VMEM((nc, rows, two), BF),
                pltpu.VMEM((nc, rows, two), BF),
                pltpu.VMEM((pc, window, two), BF),
                pltpu.VMEM((nf, window, two), BF),
                pltpu.VMEM((groups * two, vis), BF),
                pltpu.VMEM((S, vis), F32),
                pltpu.VMEM((S, vis), F32),
                pltpu.VMEM((S // 16, vis), F32),
                pltpu.VMEM((S // 16, vis), F32),
                pltpu.VMEM((2 * S, vis), BF),
                pltpu.VMEM((nf, window, two), BF),
                pltpu.VMEM((pc, window, two), BF),
                pltpu.VMEM((nc, rows, two), BF),
                pltpu.VMEM((nc, rows, two), BF),
                dma((5,)),
                dma((nc,)), dma((nc,)), dma((nf,)), dma((nf,)),
                dma((nf,)), dma((nf,)), dma((nc,)), dma((nc,)),
            ],
            compiler_params=pltpu.CompilerParams(
                collective_id=0, has_side_effects=True, vmem_limit_bytes=44 * 2**20
            ),
            name="cycle",
        )(
            fixed(facets), fixed(observed), fixed(uv_cells), fixed(counts),
            fixed(jnp.asarray(con)), fixed(jnp.asarray(scal)),
        )
        tile = 256
        return pl.pallas_call(
            functools.partial(image_kernel, nc),
            out_shape=jax.ShapeDtypeStruct((2, rows, extent), F32),
            in_specs=[vmem, vmem],
            out_specs=hbm,
            scratch_shapes=[
                pltpu.VMEM((extent // tile, 2, rows, tile), F32),
                dma((extent // tile,)),
            ],
            compiler_params=pltpu.CompilerParams(vmem_limit_bytes=16 * 2**20),
            name="image",
        )(back, tab)

    return jax.shard_map(
        on_device,
        mesh=mesh,
        in_specs=(
            P(None, ("facet", "col"), None),
            P(None, "col", None),
            P(None, "col", None),
            P("col"),
        ),
        out_specs=P(None, ("facet", "col"), None),
        check_vma=False,
    )
```

profile of v0, /device:TPU:0, one launch (start us, length us, event | category | flops | bytes accessed | tf_op | source)
XLA Modules:
  0.0 29.7 jit_solution(1708407171216576237)
XLA Ops:
  0.0 28.1 %cycle.1 = (bf16[4,256,128]{2,1,0:T(8,128)(2,1)S(1)}, bf16[2,512,1024]{2,1,0:T(8,128)(2,1)S(1)}) custom-call(bf16[2,256,1024]{2,1,0:T(8,128)(2,1)} %x_hbm.1, f32[2,8,1024]{2,1,0:T(8,128)} %obs_hbm.1, s32[2,8,1024]{2,1,0:T(8,128)} %cells_hbm.1, s32[8]{0:T(128)} %counts.1, f32[160,1024]{1,0:T(8,128)} %constant.4.clone.con_hbm, f32[9,16]{1,0:T(8,128)} %constant.5.clone.scal), custom_call_target="tpu_custom_call" | custom-call | tf_op jit(solution)/shard_map/cycle/pallas_call | solution.py:367
  28.1 1.7 %image.1 = f32[2,256,1024]{2,1,0:T(8,128)} custom-call(bf16[4,256,128]{2,1,0:T(8,128)(2,1)S(1)} %get-tuple-element.7.back, bf16[2,512,1024]{2,1,0:T(8,128)(2,1)S(1)} %get-tuple-element.8.tab), custom_call_target="tpu_custom_call" | custom-call | tf_op jit(solution)/shard_map/image/pallas_call | solution.py:409
where the time goes:
time: 30 us; the launch traced here: 29.7 us
  Pallas kernels  29.7 us (99%)
    pallas_call x1, Pallas kernels, on_device(): pl.pallas_call(functools.partial(cycle_kernel, nf, nc), out_shape=(jax.Sh...  28.1 us
    pallas_call x1, Pallas kernels, on_device(): pl.pallas_call(functools.partial(image_kernel, nc), out_shape=jax.ShapeDt...  1.65 us

commit v1 on v0

v1 whole, which is shorter than its diff:
```python
import functools
import math

import jax
import jax.numpy as jnp
import numpy as np
from jax import lax
from jax.experimental import pallas as pl
from jax.experimental.pallas import tpu as pltpu
from jax.sharding import PartitionSpec as P

S = 512
IMAGE = 65536
MESH = pl.DeviceIdType.MESH
BF = jnp.bfloat16
F32 = jnp.float32
NT = (((1,), (1,)), ((), ()))


def unit(ticks):
    angle = (np.asarray(ticks, np.int64) % IMAGE) * (-2.0 * math.pi / IMAGE)
    return np.cos(angle), np.sin(angle)


def make_constants(facets, columns, per_column, extent):
    window = S // 8
    spacing = IMAGE // extent
    cells = np.arange(extent, dtype=np.int64)
    weight = (0.6 + 0.4 * np.sin(math.pi * (cells + 0.5) / extent) ** 2) / math.sqrt(extent)
    step = np.arange(window, dtype=np.int64)
    col = np.arange(columns, dtype=np.int64)
    vc = col * (IMAGE // 4) + (29 * col + 3) % spacing
    sub = np.arange(per_column, dtype=np.int64)
    us = sub * (IMAGE // 64) + (37 * sub + 5) % (IMAGE * 8 // S)

    def table(start, stride):
        real, imag = unit((start[:, None] + stride * step)[:, :, None] * cells)
        rows = np.concatenate([real * weight, imag * weight], axis=1)
        return rows.reshape(-1, extent).astype(np.float32).astype(BF)

    col_tab = table(vc, spacing)
    wide = 2 - columns % 2
    strip_tab = col_tab.reshape(columns // wide, -1, extent).transpose(0, 2, 1)
    row_tab = table(us, IMAGE // window)
    assert extent % window == 0
    fy = extent * (np.arange(facets, dtype=np.int64) % 8)
    fx = extent * (np.arange(facets, dtype=np.int64) // 8)
    real, imag = unit((fy[:, None] * vc)[:, :, None] + (fx[:, None] * us)[:, None, :])
    same = np.stack([real, real], axis=-1)
    cross = np.stack([-imag, imag], axis=-1)
    turn = np.repeat(np.stack([same, cross], axis=3), window, axis=4)
    flat = np.ascontiguousarray
    return col_tab, flat(strip_tab), row_tab, flat(row_tab.T), turn.astype(np.float32)


def spin(value, first, second):
    half = value.shape[1] // 2
    lane = lax.broadcasted_iota(jnp.int32, value.shape, 1)
    return pltpu.roll(value, half, 1) * jnp.where(lane < half, first, second)


def sign(value, first, second):
    lane = lax.broadcasted_iota(jnp.int32, value.shape, 1)
    return value * jnp.where(lane < value.shape[1] // 2, first, second)


def cycle_kernel(
    nf, nc, x_hbm, obs_hbm, cells_hbm, counts_hbm, ctab_hbm, stab_hbm, rtab_hbm, ttab_hbm, turn_hbm,
    back_out, tab,
    xbuf, stab, obs, cells, counts, turn_in, turn_out, t2, tt, acc, bacc,
    s_send, s_recv, g_send, g_recv, right, right_t, r1r, r1i, left, obs_t, inner, held, r_send, r_recv, b_send, b_recv,
    tok, in_sem, tab_sem, sa, ra, sb, rb, sc, rc, sd, rd,
):
    f = lax.axis_index("facet")
    c = lax.axis_index("col")
    window = S // 8
    two = 2 * window
    parts = window // 16
    pc = nf
    rows = xbuf.shape[0] // 2
    groups = nf // 8
    vis = obs.shape[2]
    if nc % 2:
        col_steps = [(d, 0) for d in range(1, nc)]
        wide = 1
    else:
        col_steps = [(d, k) for d in range(nc // 2 - 1, -1, -1) for k in range(2) if d or k]
        wide = 2

    def col_at(step, sign):
        if nc % 2:
            return lax.rem(c + nc + sign * step[0], nc)
        top = lax.rem(c // 2 + nc // 2 + sign * step[0], nc // 2)
        return 2 * top + lax.rem(c + step[1], 2)

    def pair_at(q):
        return lax.rem(f // 2 + q, 4)

    def facet_link(src_buf, dst_buf, send, recv, peer, slot):
        return pltpu.make_async_remote_copy(
            src_buf.at[peer], dst_buf.at[slot], send.at[peer], recv.at[slot], (peer, c), MESH
        )

    def col_link(src_buf, dst_buf, send, recv, peer, slot):
        return pltpu.make_async_remote_copy(
            src_buf.at[peer], dst_buf.at[slot], send.at[peer], recv.at[slot], (f, peer), MESH
        )

    barrier = pltpu.get_barrier_semaphore()
    place, last_place = f // 2, nf // 2 - 1
    mate = f + 1 - 2 * lax.rem(f, 2)
    low, high = place > 0, place < last_place

    def signal(sem, facet, col):
        pl.semaphore_signal(sem, inc=1, device_id=(facet, col), device_id_type=MESH)

    inside = low & high

    def pass_on(way):
        pl.semaphore_wait(tok.at[way], 1)
        signal(tok.at[way], f + 2 - 4 * way, c)

    for d in range(1, nc):
        signal(barrier, f, lax.rem(c + d, nc))
    signal(barrier, mate, c)
    pl.when(high)(lambda: signal(barrier, f + 2, c))
    pl.when(low)(lambda: signal(barrier, f - 2, c))

    n_groups = nc // wide

    def group_at(d):
        return lax.rem(c // wide + n_groups + d, n_groups)

    group_order = list(range(n_groups - 1, -1, -1)) if wide == 2 else list(range(1, nc)) + [0]

    def tab_load(d):
        at = group_at(d)
        return pltpu.make_async_copy(stab_hbm.at[at], stab.at[at], tab_sem.at[d])

    x_loads = [
        pltpu.make_async_copy(x_hbm.at[k], xbuf.at[k * rows : (k + 1) * rows], in_sem.at[k])
        for k in range(2)
    ]
    row_load = pltpu.make_async_copy(rtab_hbm, t2, in_sem.at[2])
    small_loads = [
        pltpu.make_async_copy(turn_hbm.at[f, c], turn_in, in_sem.at[3]),
        pltpu.make_async_copy(turn_hbm.at[:, c, f], turn_out, in_sem.at[4]),
        pltpu.make_async_copy(obs_hbm, obs, in_sem.at[5]),
        pltpu.make_async_copy(cells_hbm, cells, in_sem.at[6]),
        pltpu.make_async_copy(counts_hbm, counts, in_sem.at[7]),
    ]
    image_load = pltpu.make_async_copy(ctab_hbm, tab, in_sem.at[9])
    back_load = pltpu.make_async_copy(ttab_hbm, tt, in_sem.at[8])
    for n, d in enumerate(group_order):
        tab_load(d).start()
        if n == 0:
            for load in x_loads:
                load.start()
    for load in small_loads:
        load.start()

    pl.semaphore_wait(barrier, nc + low.astype(jnp.int32) + high.astype(jnp.int32))
    pl.when(~low)(lambda: signal(tok.at[0], f + 2, c))
    pl.when(~high)(lambda: signal(tok.at[1], f - 2, c))

    for load in x_loads:
        load.wait()
    row_load.start()
    for n, d in enumerate(group_order):
        start = wide * group_at(d)
        tab_load(d).wait()
        both = jnp.dot(xbuf[...], stab[group_at(d)], preferred_element_type=F32)
        for k in range(wide):
            block = both[:, k * two : (k + 1) * two]
            s_send[start + k] = (block[:rows] + spin(block[rows:], -1.0, 1.0)).astype(BF)
        for step in col_steps:
            if step[0] == d:
                peer = col_at(step, 1)
                col_link(s_send, s_recv, sa, ra, peer, c).start()
        if n == 0:
            pl.when(inside & (place == last_place - 1))(functools.partial(pass_on, 1))
    pl.when(inside & (place == 1))(functools.partial(pass_on, 0))

    row_load.wait()

    def part_product(src, block, at, count):
        start = pl.multiple_of(src * rows, rows)
        return jnp.dot(
            t2[pl.ds(at, count), pl.ds(start, rows)], block, preferred_element_type=F32
        )

    acc[...] = part_product(c, s_send[c], 0, pc * two)

    pl.when(inside & (place != 1))(functools.partial(pass_on, 0))
    pl.when(inside & (place != last_place - 1))(functools.partial(pass_on, 1))

    for load in small_loads:
        load.wait()
    first = cells[0, pl.ds(f, 1), :]
    second = cells[1, pl.ds(f, 1), :]

    def wave(count, step, cell):
        index = step * lax.broadcasted_iota(jnp.int32, (count, vis), 0)
        angle = (index * cell & (S - 1)).astype(F32) * (-2.0 * math.pi / S)
        return jnp.cos(angle), jnp.sin(angle)

    scale = 1.0 / math.sqrt(vis)
    live = lax.broadcasted_iota(jnp.int32, (1, vis), 1) < counts[f]
    gain = jnp.where(live, scale, 0.0)
    m0r, m0i = wave(16, 1, second)
    m0r, m0i = m0r * gain, m0i * gain
    r1r[...], r1i[...] = wave(S // 16, 16, second)

    def right_body(i, carry):
        er, ei = r1r[pl.ds(i, 1), :], r1i[pl.ds(i, 1), :]
        b = i // parts
        at = pl.multiple_of(b * two + (i - b * parts) * 16, 16)
        right[pl.ds(at, 16), :] = (m0r * er - m0i * ei).astype(BF)
        right[pl.ds(at + window, 16), :] = (m0r * ei + m0i * er).astype(BF)
        return carry

    lax.fori_loop(0, S // 16, right_body, 0)

    def turn_body(i, carry):
        at = pl.multiple_of(i * two, two)
        block = right[pl.ds(at, two), :].astype(F32) * (1.0 / (scale * S))
        right_t[:, pl.ds(at, two)] = block.T.astype(BF)
        return carry

    lax.fori_loop(0, S // window, turn_body, 0)

    for step in col_steps[:0:-1]:
        src = col_at(step, -1)
        col_link(s_send, s_recv, sa, ra, src, src).wait_recv()
        acc[...] += part_product(src, s_recv[src], 0, pc * two)

    def each_facet(q, act):
        pair = pair_at(q)
        for g in range(groups):
            for h in range(2):
                index = g * 8 + 2 * pair + h
                if q == 0:
                    pl.when(index != f)(functools.partial(act, index))
                else:
                    act(index)

    def send_window(index):
        facet_link(g_send, g_recv, sb, rb, index, f).start()

    def take_window(index):
        facet_link(g_send, g_recv, sb, rb, index, index).wait_recv()

    def send_back(index):
        facet_link(r_send, r_recv, sc, rc, index, f).start()

    def take_back(index):
        facet_link(r_send, r_recv, sc, rc, index, index).wait_recv()

    far_first = (2, 3, 1, 0)
    src = col_at(col_steps[0], -1)
    col_link(s_send, s_recv, sa, ra, src, src).wait_recv()
    pl.when(~low)(lambda: pl.semaphore_wait(tok.at[1], 1))
    pl.when(~high)(lambda: pl.semaphore_wait(tok.at[0], 1))
    total = acc[...] + part_product(src, s_recv[src], 0, pc * two)
    for j in range(pc):
        u = total[j * two : j * two + window]
        v = total[j * two + window : (j + 1) * two]
        turn = turn_in[j]
        same, cross = turn[0:1], turn[1:2]
        win = u * same + spin(v, -1.0, 1.0) * same
        win += pltpu.roll(u, window, 1) * cross + v * sign(cross, 1.0, -1.0)
        g_send[j] = win.astype(BF)
    for q in far_first:
        each_facet(q, send_window)
    g_recv[f] = g_send[f]
    back_load.start()
    image_load.start()

    l0r, l0i = wave(16, 1, first)
    l1r, l1i = wave(max(groups * parts, 8), 16, first)
    for g in range(groups):
        reals, imags = [], []
        for k in range(parts):
            i = g * parts + k
            er, ei = l1r[i : i + 1], l1i[i : i + 1]
            reals.append(l0r * er - l0i * ei)
            imags.append(-(l0r * ei + l0i * er))
        turned = jnp.concatenate(reals + imags, axis=0).astype(BF).astype(F32)
        turned = turned.T
        left[0, :, g * two : (g + 1) * two] = turned
        left[1, :, g * two : (g + 1) * two] = spin(turned, -1.0, 1.0)
    for k in range(2):
        obs_t[k] = jnp.broadcast_to(obs[k, pl.ds(f, 1), :], (two, vis)).T

    def pred_chunk(q, g):
        pieces = []
        for h in range(2):
            block = g_recv[g * 8 + 2 * pair_at(q) + h].astype(F32)
            pieces.append(
                jnp.concatenate([sign(block, 1.0, -1.0), pltpu.roll(block, window, 1)], axis=0)
            )
        lanes = pl.multiple_of(pair_at(q) * 2 * two, 2 * two)
        return lax.dot_general(
            right_t[:, pl.ds(lanes, 2 * two)],
            jnp.concatenate(pieces, axis=1).astype(BF),
            NT,
            preferred_element_type=F32,
        )

    nearest = far_first[::-1]
    for q in nearest[:-1]:
        each_facet(q, take_window)
        for g in range(groups):
            at = slice(g * two, (g + 1) * two)
            if q == nearest[0]:
                inner[:, at] = pred_chunk(q, g)
            else:
                inner[:, at] += pred_chunk(q, g)
    each_facet(nearest[-1], take_window)
    ones = jnp.ones((two, two), BF)
    rest = [obs_t[0], obs_t[1]]
    for g in range(groups):
        at = slice(g * two, (g + 1) * two)
        value = inner[:, at] + pred_chunk(nearest[-1], g)
        for k in range(2):
            rest[k] -= jnp.dot(
                (value * left[k, :, at]).astype(BF), ones, preferred_element_type=F32
            )
    for g in range(groups):
        at = slice(g * two, (g + 1) * two)
        held[:, at] = (rest[0] * left[0, :, at] + rest[1] * left[1, :, at]).astype(BF)

    for n, q in enumerate(far_first):
        at = pl.multiple_of(pair_at(q) * 2 * two, 2 * two)
        grid = jnp.dot(right[pl.ds(at, 2 * two), :], held[...], preferred_element_type=F32)
        for g in range(groups):
            lanes = slice(g * two, (g + 1) * two)
            for h in range(2):
                u = grid[h * two : h * two + window, lanes]
                v = grid[h * two + window : (h + 1) * two, lanes]
                index = g * 8 + 2 * pair_at(q) + h
                turn = turn_out[index]
                same, cross = turn[0:1], turn[1:2]
                block = (u + spin(v, 1.0, -1.0)) * same
                block -= pltpu.roll(u, window, 1) * cross + v * sign(cross, -1.0, 1.0)
                r_send[index] = block.astype(BF)
        if n % 2:
            for far in far_first[n - 1 : n + 1]:
                each_facet(far, send_back)
    r_recv[f] = r_send[f]

    back_load.wait()
    image_load.wait()

    def back_chunk(q, g):
        first = g * 8 + 2 * pair_at(q)
        pieces = []
        for h in range(2):
            ret = r_recv[first + h]
            other = spin(ret.astype(F32), 1.0, -1.0).astype(BF)
            pieces.append(jnp.concatenate([ret, other], axis=0))
        return pl.multiple_of(first * two, 2 * two), jnp.concatenate(pieces, axis=1)

    for q in nearest[:-1]:
        each_facet(q, take_back)
        for g in range(groups):
            at, chunk = back_chunk(q, g)
            term = lax.dot_general(
                tt[:, pl.ds(at, 2 * two)], chunk, NT, preferred_element_type=F32
            )
            if q == nearest[0] and g == 0:
                bacc[...] = term
            else:
                bacc[...] += term
    each_facet(nearest[-1], take_back)
    chunks = [back_chunk(nearest[-1], g) for g in range(groups)]

    def back_strip(cp):
        at = pl.ds(pl.multiple_of(cp * rows, rows), rows)
        strip = bacc[at]
        for lane, chunk in chunks:
            strip += lax.dot_general(
                tt[at, pl.ds(lane, 2 * two)], chunk, NT, preferred_element_type=F32
            )
        return strip.astype(BF)

    for step in col_steps:
        peer = col_at(step, 1)
        b_send[peer] = back_strip(peer)
        col_link(b_send, b_recv, sd, rd, peer, c).start()
    back_out[c] = back_strip(c)
    for step in col_steps[::-1]:
        src = col_at(step, -1)
        col_link(b_send, b_recv, sd, rd, src, src).wait_recv()
        back_out[src] = b_recv[src]
    for step in col_steps:
        peer = col_at(step, 1)
        col_link(s_send, s_recv, sa, ra, peer, c).wait_send()
        col_link(b_send, b_recv, sd, rd, peer, c).wait_send()
    for d in range(1, nf):
        peer = lax.rem(f + d, nf)
        facet_link(g_send, g_recv, sb, rb, peer, f).wait_send()
        facet_link(r_send, r_recv, sc, rc, peer, f).wait_send()


def image_kernel(nc, back, tab, out, buf, sem):
    tiles, rows, tile = buf.shape[0], buf.shape[2], buf.shape[3]
    strip = jnp.concatenate([back[k] for k in range(nc)], axis=1)
    spun = [spin(back[k].astype(F32), 1.0, -1.0).astype(BF) for k in range(nc)]
    strip = jnp.concatenate([strip, jnp.concatenate(spun, axis=1)], axis=0)
    stores = []
    for t in range(tiles):
        piece = jnp.dot(strip, tab[:, t * tile : (t + 1) * tile], preferred_element_type=F32)
        for part in range(2):
            buf[t, part] = piece[part * rows : (part + 1) * rows]
        store = pltpu.make_async_copy(
            buf.at[t], out.at[:, :, t * tile : (t + 1) * tile], sem.at[t]
        )
        store.start()
        stores.append(store)
    for store in stores:
        store.wait()


def solution(mesh):
    nf, nc = mesh.shape["facet"], mesh.shape["col"]

    def on_device(facets, observed, uv_cells, counts):
        rows, extent = facets.shape[1:]
        vis = observed.shape[2]
        pc = counts.shape[0]
        window = S // 8
        two = 2 * window
        groups = nf // 8
        assert pc == nf and nf % 8 == 0 and nf <= 32
        constants = make_constants(nf, nc, pc, extent)
        vmem = pl.BlockSpec(memory_space=pltpu.VMEM)
        hbm = pl.BlockSpec(memory_space=pltpu.HBM)
        dma = pltpu.SemaphoreType.DMA
        fixed = functools.partial(pltpu.with_memory_space_constraint, memory_space=pltpu.HBM)
        back, tab = pl.pallas_call(
            functools.partial(cycle_kernel, nf, nc),
            out_shape=(
                jax.ShapeDtypeStruct((nc, rows, two), BF),
                jax.ShapeDtypeStruct((nc * two, extent), BF),
            ),
            in_specs=[hbm] * 9,
            out_specs=(vmem, vmem),
            scratch_shapes=[
                pltpu.VMEM((2 * rows, extent), BF),
                pltpu.VMEM(constants[1].shape, BF),
                pltpu.VMEM((2, pc, vis), F32),
                pltpu.VMEM((2, pc, vis), jnp.int32),
                pltpu.SMEM((pc,), jnp.int32),
                pltpu.VMEM((pc, 2, two), F32),
                pltpu.VMEM((nf, 2, two), F32),
                pltpu.VMEM((pc * two, extent), BF),
                pltpu.VMEM((extent, pc * two), BF),
                pltpu.VMEM((pc * two, two), F32),
                pltpu.VMEM((extent, two), F32),
                pltpu.VMEM((nc, rows, two), BF),
                pltpu.VMEM((nc, rows, two), BF),
                pltpu.VMEM((pc, window, two), BF),
                pltpu.VMEM((nf, window, two), BF),
                pltpu.VMEM((2 * S, vis), BF),
                pltpu.VMEM((vis, 2 * S), BF),
                pltpu.VMEM((S // 16, vis), F32),
                pltpu.VMEM((S // 16, vis), F32),
                pltpu.VMEM((2, vis, groups * two), F32),
                pltpu.VMEM((2, vis, two), F32),
                pltpu.VMEM((vis, groups * two), F32),
                pltpu.VMEM((vis, groups * two), BF),
                pltpu.VMEM((nf, window, two), BF),
                pltpu.VMEM((pc, window, two), BF),
                pltpu.VMEM((nc, rows, two), BF),
                pltpu.VMEM((nc, rows, two), BF),
                pltpu.SemaphoreType.REGULAR((2,)),
                dma((10,)), dma((nc,)),
                dma((nc,)), dma((nc,)), dma((nf,)), dma((nf,)),
                dma((nf,)), dma((nf,)), dma((nc,)), dma((nc,)),
            ],
            compiler_params=pltpu.CompilerParams(
                collective_id=0, has_side_effects=True, vmem_limit_bytes=44 * 2**20
            ),
            name="cycle",
        )(
            fixed(facets), fixed(observed), fixed(uv_cells), fixed(counts),
            *(fixed(jnp.asarray(constant)) for constant in constants),
        )
        tile = 256
        return pl.pallas_call(
            functools.partial(image_kernel, nc),
            out_shape=jax.ShapeDtypeStruct((2, rows, extent), F32),
            in_specs=[vmem, vmem],
            out_specs=hbm,
            scratch_shapes=[
                pltpu.VMEM((extent // tile, 2, rows, tile), F32),
                dma((extent // tile,)),
            ],
            compiler_params=pltpu.CompilerParams(vmem_limit_bytes=16 * 2**20),
            name="image",
        )(back, tab)

    return jax.shard_map(
        on_device,
        mesh=mesh,
        in_specs=(
            P(None, ("facet", "col"), None),
            P(None, "col", None),
            P(None, "col", None),
            P("col"),
        ),
        out_specs=P(None, ("facet", "col"), None),
        check_vma=False,
    )
```

time: 30 us -> 29.2 us (0.973)
  Pallas kernels: 29.7 us -> 29 us
    pallas_call x1, Pallas kernels: 28.1 us -> 27.2 us  [on_device(): pl.pallas_call(functools.partial(cycle_kernel, nf, nc), out_shape=(jax.Sh...]
where the time goes in v1:
time: 29.2 us; the launch traced here: 29 us
  Pallas kernels  29 us (99%)
    pallas_call x1, Pallas kernels, on_device(): pl.pallas_call(functools.partial(cycle_kernel, nf, nc), out_shape=(jax.Sh...  27.2 us
    pallas_call x1, Pallas kernels, on_device(): pl.pallas_call(functools.partial(image_kernel, nc), out_shape=jax.ShapeDt...  1.79 us

profile of v1, /device:TPU:0, one launch (start us, length us, event | category | flops | bytes accessed | tf_op | source)
XLA Modules:
  0.0 29.0 jit_solution(579149828359496420)
XLA Ops:
  0.0 27.2 %cycle.1 = (bf16[4,256,128]{2,1,0:T(8,128)(2,1)S(1)}, bf16[512,1024]{1,0:T(8,128)(2,1)S(1)}) custom-call(bf16[2,256,1024]{2,1,0:T(8,128)(2,1)} %x_hbm.1, f32[2,8,1024]{2,1,0:T(8,128)} %obs_hbm.1, s32[2,8,1024]{2,1,0:T(8,128)} %cells_hbm.1, s32[8]{0:T(128)} %counts_hbm.1, bf16[512,1024]{1,0:T(8,128)(2,1)} %constant.10.clone.ctab_hbm, ...), custom_call_target="tpu_custom_call" | custom-call | tf_op jit(solution)/shard_map/cycle/pallas_call | solution.py:441
  27.2 1.8 %image.1 = f32[2,256,1024]{2,1,0:T(8,128)} custom-call(bf16[4,256,128]{2,1,0:T(8,128)(2,1)S(1)} %get-tuple-element.7.back, bf16[512,1024]{1,0:T(8,128)(2,1)S(1)} %get-tuple-element.8.tab), custom_call_target="tpu_custom_call" | custom-call | tf_op jit(solution)/shard_map/image/pallas_call | solution.py:491

commit v2 on v1

v2 whole, which is shorter than its diff:
```python
import functools
import math

import jax
import jax.numpy as jnp
import numpy as np
from jax import lax
from jax.experimental import pallas as pl
from jax.experimental.pallas import tpu as pltpu
from jax.sharding import PartitionSpec as P

S = 512
IMAGE = 65536
MESH = pl.DeviceIdType.MESH
BF = jnp.bfloat16
F32 = jnp.float32
NT = (((1,), (1,)), ((), ()))


def unit(ticks):
    angle = (np.asarray(ticks, np.int64) % IMAGE) * (-2.0 * math.pi / IMAGE)
    return np.cos(angle), np.sin(angle)


def make_constants(facets, columns, per_column, extent):
    window = S // 8
    spacing = IMAGE // extent
    cells = np.arange(extent, dtype=np.int64)
    weight = (0.6 + 0.4 * np.sin(math.pi * (cells + 0.5) / extent) ** 2) / math.sqrt(extent)
    step = np.arange(window, dtype=np.int64)
    col = np.arange(columns, dtype=np.int64)
    vc = col * (IMAGE // 4) + (29 * col + 3) % spacing
    sub = np.arange(per_column, dtype=np.int64)
    us = sub * (IMAGE // 64) + (37 * sub + 5) % (IMAGE * 8 // S)

    def table(start, stride):
        real, imag = unit((start[:, None] + stride * step)[:, :, None] * cells)
        return np.stack([real * weight, imag * weight], axis=1).astype(np.float32).astype(BF)

    wide = 2 - columns % 2
    col_tab = table(vc, spacing).reshape(columns // wide, wide, 2, 2, window // 2, extent)
    col_tab = col_tab.transpose(0, 3, 1, 2, 4, 5).reshape(-1, extent)
    row_tab = table(us, IMAGE // window).reshape(-1, extent)
    assert extent % window == 0
    fy = extent * (np.arange(facets, dtype=np.int64) % 8)
    fx = extent * (np.arange(facets, dtype=np.int64) // 8)
    real, imag = unit((fy[:, None] * vc)[:, :, None] + (fx[:, None] * us)[:, None, :])
    same = np.stack([real, real], axis=-1)
    cross = np.stack([-imag, imag], axis=-1)
    turn = np.repeat(np.stack([same, cross], axis=3), window, axis=4)
    flat = np.ascontiguousarray
    return flat(col_tab), row_tab, flat(row_tab.T), turn.astype(np.float32)


def spin(value, first, second):
    half = value.shape[1] // 2
    lane = lax.broadcasted_iota(jnp.int32, value.shape, 1)
    return pltpu.roll(value, half, 1) * jnp.where(lane < half, first, second)


def sign(value, first, second):
    lane = lax.broadcasted_iota(jnp.int32, value.shape, 1)
    return value * jnp.where(lane < value.shape[1] // 2, first, second)


def image_rows(blocks):
    half = blocks[0].shape[0] // 2
    cross = []
    for block in blocks:
        cross += [block[half:], -block[:half]]
    return jnp.concatenate(
        [jnp.concatenate(blocks, axis=0).T, jnp.concatenate(cross, axis=0).T], axis=0
    )


def cycle_kernel(
    nf, nc, x_hbm, obs_hbm, cells_hbm, counts_hbm, ctab_hbm, rtab_hbm, ttab_hbm, turn_hbm,
    back_out, base_out, tab,
    xbuf, obs, cells, counts, turn_in, turn_out, t2, tt, acc, bacc,
    s_send, s_recv, g_send, g_recv, right, right_t, r1r, r1i, left, inner, held,
    r_send, r_recv, b_send, b_recv,
    tok, in_sem, tab_sem, sa, ra, sb, rb, sc, rc, sd, rd,
):
    f = lax.axis_index("facet")
    c = lax.axis_index("col")
    window = S // 8
    half = window // 2
    two = 2 * window
    parts = window // 16
    pc = nf
    rows = xbuf.shape[0] // 2
    groups = nf // 8
    vis = obs.shape[2]
    if nc % 2:
        col_steps = [(d, 0) for d in range(1, nc)]
        wide = 1
    else:
        col_steps = [(d, k) for d in range(nc // 2 - 1, -1, -1) for k in range(2) if d or k]
        wide = 2
    near_steps = [step for step in col_steps if step[0] == 0]
    far_steps = [step for step in col_steps if step[0]]

    def col_at(step, sign):
        if nc % 2:
            return lax.rem(c + nc + sign * step[0], nc)
        top = lax.rem(c // 2 + nc // 2 + sign * step[0], nc // 2)
        return 2 * top + lax.rem(c + step[1], 2)

    def pair_at(q):
        return lax.rem(f // 2 + q, 4)

    def group_of(q):
        return 0 if q in waits[0] else 1

    def facet_link(src_buf, dst_buf, send, recv, part, peer, slot, group):
        return pltpu.make_async_remote_copy(
            src_buf.at[part, peer], dst_buf.at[part, slot],
            send.at[part], recv.at[part, group], (peer, c), MESH,
        )

    def col_link(src_buf, dst_buf, send, recv, part, peer, slot):
        return pltpu.make_async_remote_copy(
            src_buf.at[part, peer], dst_buf.at[part, slot], send.at[part], recv, (f, peer), MESH
        )

    def sum_of(buf, part, count, send, recv):
        some = buf.at[part, 0:count]
        return pltpu.make_async_remote_copy(some, some, send, recv, (mate, c), MESH)

    waits = ((0, 1), (3, 2))
    mate = f + 1 - 2 * lax.rem(f, 2)

    barrier = pltpu.get_barrier_semaphore()
    place, last_place = f // 2, nf // 2 - 1
    low, high = place > 0, place < last_place

    def signal(sem, facet, col):
        pl.semaphore_signal(sem, inc=1, device_id=(facet, col), device_id_type=MESH)

    inside = low & high

    def pass_on(way):
        pl.semaphore_wait(tok.at[way], 1)
        signal(tok.at[way], f + 2 - 4 * way, c)

    for d in range(1, nc):
        signal(barrier, f, lax.rem(c + d, nc))
    signal(barrier, mate, c)
    pl.when(high)(lambda: signal(barrier, f + 2, c))
    pl.when(low)(lambda: signal(barrier, f - 2, c))

    n_groups = nc // wide
    chunk = wide * window

    def group_at(d):
        return lax.rem(c // wide + n_groups + d, n_groups)

    far_groups = list(range(n_groups - 1, 0, -1)) if wide == 2 else list(range(1, nc))

    def tab_load(d):
        at = pl.ds(pl.multiple_of(group_at(d) * 2 * chunk, 2 * chunk), 2 * chunk)
        return pltpu.make_async_copy(ctab_hbm.at[at], tab.at[at], tab_sem.at[d])

    x_loads = [
        pltpu.make_async_copy(x_hbm.at[k], xbuf.at[k * rows : (k + 1) * rows], in_sem.at[k])
        for k in range(2)
    ]
    row_load = pltpu.make_async_copy(rtab_hbm, t2, in_sem.at[2])
    small_loads = [
        pltpu.make_async_copy(turn_hbm.at[f, c], turn_in, in_sem.at[3]),
        pltpu.make_async_copy(turn_hbm.at[:, c, f], turn_out, in_sem.at[4]),
        pltpu.make_async_copy(obs_hbm, obs, in_sem.at[5]),
        pltpu.make_async_copy(cells_hbm, cells, in_sem.at[6]),
        pltpu.make_async_copy(counts_hbm, counts, in_sem.at[7]),
    ]
    turned_load = pltpu.make_async_copy(ttab_hbm, tt, in_sem.at[8])
    for n, d in enumerate(far_groups + [0]):
        tab_load(d).start()
        if n == 0:
            for load in x_loads:
                load.start()
    for load in small_loads:
        load.start()

    pl.semaphore_wait(barrier, nc + low.astype(jnp.int32) + high.astype(jnp.int32))
    pl.when(~low)(lambda: signal(tok.at[0], f + 2, c))
    pl.when(~high)(lambda: signal(tok.at[1], f - 2, c))

    for load in x_loads:
        load.wait()
    turned_load.start()

    def strips(d, first_part, n_parts):
        at = pl.multiple_of(group_at(d) * 2 * chunk + first_part * chunk, chunk)
        both = lax.dot_general(
            tab[pl.ds(at, n_parts * chunk), :], xbuf[...], NT, preferred_element_type=F32
        )
        for part in range(n_parts):
            for k in range(wide):
                at = part * chunk + k * window
                real, imag = both[at : at + half], both[at + half : at + window]
                block = [real[:, :rows] - imag[:, rows:], imag[:, :rows] + real[:, rows:]]
                s_send[first_part + part, wide * group_at(d) + k] = jnp.concatenate(
                    block, axis=0
                ).astype(BF)

    def send_strips(d, part):
        for n, step in enumerate(col_steps):
            if step[0] == d:
                at = part * len(col_steps) + n
                col_link(s_send, s_recv, sa, ra.at[at], part, col_at(step, 1), c).start()

    for n, d in enumerate(far_groups):
        tab_load(d).wait()
    for part in range(2):
        for d in far_groups:
            strips(d, part, 1)
            send_strips(d, part)
    pl.when(inside & (place == last_place - 1))(functools.partial(pass_on, 1))
    tab_load(0).wait()
    strips(0, 0, 2)
    for part in range(2):
        send_strips(0, part)
    pl.when(inside & (place == 1))(functools.partial(pass_on, 0))

    turned_load.wait()

    def window_term(block, src):
        at = pl.multiple_of(src * rows, rows)
        return jnp.dot(block, tt[pl.ds(at, rows), :], preferred_element_type=F32)

    acc[...] = window_term(jnp.concatenate([s_send[0, c], s_send[1, c]], axis=0), c)
    pl.when(inside & (place != 1))(functools.partial(pass_on, 0))
    pl.when(inside & (place != last_place - 1))(functools.partial(pass_on, 1))

    for load in small_loads:
        load.wait()

    def each_facet(q, act):
        pair = pair_at(q)
        for g in range(groups):
            for h in range(2):
                index = g * 8 + 2 * pair + h
                if q == 0:
                    pl.when(index != f)(functools.partial(act, index))
                else:
                    act(index)

    def send_facets(src_buf, dst_buf, send, recv, part):
        for q in far_first:
            each_facet(
                q,
                lambda index, q=q: facet_link(
                    src_buf, dst_buf, send, recv, part, index, f, group_of(-q % 4)
                ).start(),
            )
        dst_buf[part, f] = src_buf[part, f]

    def take_facets(buf, send, recv, part, pairs):
        for group in range(2):
            if waits[group][0] in pairs:
                count = 4 * groups - (0 in waits[group])
                sum_of(buf, part, count, send.at[part], recv.at[part, group]).wait_recv()

    far_first = (2, 3, 1, 0)

    def take_strip(part, step):
        src = col_at(step, -1)
        at = part * len(col_steps) + col_steps.index(step)
        col_link(s_send, s_recv, sa, ra.at[at], part, src, src).wait_recv()

    for step in near_steps:
        src = col_at(step, -1)
        for part in range(2):
            take_strip(part, step)
        acc[...] += window_term(jnp.concatenate([s_recv[0, src], s_recv[1, src]], axis=0), src)

    def windows(part):
        total = acc[part * window : (part + 1) * window]
        for step in far_steps:
            src = col_at(step, -1)
            take_strip(part, step)
            total += window_term(s_recv[part, src], src)
        for j in range(pc):
            u = total[:half, j * two : (j + 1) * two]
            v = total[half:, j * two : (j + 1) * two]
            turn = turn_in[j]
            same, cross = turn[0:1], turn[1:2]
            win = u * same + spin(v, -1.0, 1.0) * same
            win += pltpu.roll(u, window, 1) * cross + v * sign(cross, 1.0, -1.0)
            g_send[part, j] = win.astype(BF)
        if part == 0:
            pl.when(~low)(lambda: pl.semaphore_wait(tok.at[1], 1))
            pl.when(~high)(lambda: pl.semaphore_wait(tok.at[0], 1))
        send_facets(g_send, g_recv, sb, rb, part)

    windows(0)

    first = cells[0, pl.ds(f, 1), :]
    second = cells[1, pl.ds(f, 1), :]

    def series(square, first, terms):
        value = jnp.full_like(square, 1.0 / math.factorial(first + 2 * terms))
        for k in range(terms - 1, -1, -1):
            value = 1.0 / math.factorial(first + 2 * k) - value * square
        return value

    def wave(count, step, cell):
        index = step * lax.broadcasted_iota(jnp.int32, (count, vis), 0)
        turn = ((index * cell + S // 2) & (S - 1)) - S // 2
        angle = turn.astype(F32) * (-math.pi / S)
        square = angle * angle
        sine = angle * series(square, 1, 5)
        return 1.0 - 2.0 * sine * sine, 2.0 * sine * series(square, 0, 6)

    scale = 1.0 / math.sqrt(vis)
    live = lax.broadcasted_iota(jnp.int32, (1, vis), 1) < counts[f]
    gain = jnp.where(live, scale, 0.0)
    m0r, m0i = wave(16, 1, second)
    m0r, m0i = m0r * gain, m0i * gain
    r1r[...], r1i[...] = wave(S // 16, 16, second)

    def right_body(i, carry):
        er, ei = r1r[pl.ds(i, 1), :], r1i[pl.ds(i, 1), :]
        b = i // parts
        k = i - b * parts
        h = k // (parts // 2)
        at = pl.multiple_of(h * S + b * window + (k - h * (parts // 2)) * 16, 16)
        right[pl.ds(at, 16), :] = (m0r * er - m0i * ei).astype(BF)
        right[pl.ds(at + half, 16), :] = (m0r * ei + m0i * er).astype(BF)
        return carry

    lax.fori_loop(0, S // 16, right_body, 0)

    windows(1)
    row_load.start()

    def turn_body(i, carry):
        at = pl.multiple_of(i * two, two)
        right_t[:, pl.ds(at, two)] = right[pl.ds(at, two), :].T
        return carry

    lax.fori_loop(0, S // window, turn_body, 0)

    l0r, l0i = wave(16, 1, first)
    l1r, l1i = wave(max(groups * parts, 8), 16, first)
    for i in range(groups * parts):
        er, ei = l1r[i : i + 1], l1i[i : i + 1]
        at = i // parts * two + i % parts * 16
        real = (l0r * er - l0i * ei).astype(BF).astype(F32)
        imag = (l0r * ei + l0i * er).astype(BF).astype(F32)
        left[0, at : at + 16, :] = real
        left[0, at + window : at + window + 16, :] = -imag
        left[1, at : at + 16, :] = imag
        left[1, at + window : at + window + 16, :] = real

    def pred_term(part, pairs, g):
        blocks, tables = [], []
        for q in pairs:
            for h in range(2):
                block = g_recv[part, g * 8 + 2 * pair_at(q) + h].astype(F32)
                blocks += [block, spin(block, -1.0, 1.0)]
            at = pl.multiple_of(part * S + pair_at(q) * two, two)
            tables.append(right[pl.ds(at, two), :])
        return jnp.dot(
            jnp.concatenate(blocks, axis=0).T.astype(BF),
            jnp.concatenate(tables, axis=0),
            preferred_element_type=F32,
        )

    for part in range(2):
        for pairs in waits if part else (waits[0] + waits[1],):
            take_facets(g_recv, sb, rb, part, pairs)
            if pairs == waits[1]:
                continue
            for g in range(groups):
                at = slice(g * two, (g + 1) * two)
                if part == 0:
                    inner[at] = pred_term(part, pairs, g)
                else:
                    inner[at] += pred_term(part, pairs, g)
    res_r, res_i = obs[0, pl.ds(f, 1), :], obs[1, pl.ds(f, 1), :]
    for g in range(groups):
        at = slice(g * two, (g + 1) * two)
        value = inner[at] + pred_term(1, waits[-1], g)
        unscale = 1.0 / (scale * S)
        res_r -= jnp.sum(value * left[0, at], axis=0, keepdims=True) * unscale
        res_i -= jnp.sum(value * left[1, at], axis=0, keepdims=True) * unscale
    held[...] = (res_r * left[0] + res_i * left[1]).astype(BF)

    for part in range(2):
        grid = jnp.dot(
            held[...], right_t[:, part * S : (part + 1) * S], preferred_element_type=F32
        )
        for g in range(groups):
            block_t = grid[g * two : (g + 1) * two].T
            for b in range(8):
                u = block_t[b * window : b * window + half]
                v = block_t[b * window + half : (b + 1) * window]
                turn = turn_out[g * 8 + b]
                same, cross = turn[0:1], turn[1:2]
                block = (u + spin(v, 1.0, -1.0)) * same
                block -= pltpu.roll(u, window, 1) * cross + v * sign(cross, -1.0, 1.0)
                r_send[part, g * 8 + b] = block.astype(BF)
        send_facets(r_send, r_recv, sc, rc, part)

    row_load.wait()

    def back_term(part, pairs):
        total = None
        take_facets(r_recv, sc, rc, part, pairs)
        for q in pairs:
            for g in range(groups):
                first = g * 8 + 2 * pair_at(q)
                pieces = [r_recv[part, first + h] for h in range(2)]
                spun = [spin(piece.astype(F32), 1.0, -1.0).astype(BF) for piece in pieces]
                block = jnp.concatenate(
                    [jnp.concatenate(pieces, axis=1), jnp.concatenate(spun, axis=1)], axis=0
                )
                at = pl.multiple_of(first * two, 2 * two)
                term = jnp.dot(block, t2[pl.ds(at, 2 * two), :], preferred_element_type=F32)
                total = term if total is None else total + term
        return total

    def back_strips(part):
        total = (bacc[...] + back_term(part, waits[1])).astype(BF)
        for cp in range(nc):
            b_send[part, cp] = total[:, cp * rows : (cp + 1) * rows]
        for step in col_steps:
            at = rd.at[0 if step in near_steps else 1 + part]
            col_link(b_send, b_recv, sd, at, part, col_at(step, 1), c).start()
        b_recv[part, c] = b_send[part, c]

    bacc[...] = back_term(0, waits[0])
    back_strips(0)
    bacc[...] = back_term(1, waits[0])
    back_strips(1)
    if near_steps:
        sum_of(b_recv, 0, 2 * len(near_steps), sd.at[0], rd.at[0]).wait_recv()
    mine = [b_recv[part, wide * group_at(0) + k] for part in range(2) for k in range(wide)]
    at = pl.multiple_of(group_at(0) * 2 * chunk, 2 * chunk)
    base_out[...] = jnp.dot(
        image_rows(mine), tab[pl.ds(at, 2 * chunk), :], preferred_element_type=F32
    )
    sum_of(b_recv, 0, len(far_steps), sd.at[0], rd.at[1]).wait_recv()
    sum_of(b_recv, 1, len(far_steps), sd.at[1], rd.at[2]).wait_recv()
    for part in range(2):
        for d in range(1, n_groups):
            for k in range(wide):
                back_out[((d - 1) * 2 + part) * wide + k] = b_recv[part, wide * group_at(d) + k]
    for part in range(2):
        sum_of(s_send, part, nc - 1, sa.at[part], rd.at[0]).wait_send()
        sum_of(b_send, part, nc - 1, sd.at[part], rd.at[0]).wait_send()
        sum_of(g_send, part, nf - 1, sb.at[part], rb.at[0, 0]).wait_send()
        sum_of(r_send, part, nf - 1, sc.at[part], rc.at[0, 0]).wait_send()


def image_kernel(nc, back, base, tab, out, buf, sem):
    c = lax.axis_index("col")
    wide = 2 - nc % 2
    n_groups = nc // wide
    tiles, rows, tile = buf.shape[0], buf.shape[2], buf.shape[3]
    depth = 2 * wide * back.shape[1]
    strip = image_rows([back[k] for k in range(back.shape[0])])
    stores = []
    for t in range(tiles):
        lanes = slice(t * tile, (t + 1) * tile)
        piece = base[:, lanes]
        for d in range(1, n_groups):
            at = pl.multiple_of(lax.rem(c // wide + d, n_groups) * depth, depth)
            piece += jnp.dot(
                strip[:, (d - 1) * depth : d * depth],
                tab[pl.ds(at, depth), lanes],
                preferred_element_type=F32,
            )
        for part in range(2):
            buf[t, part] = piece[part * rows : (part + 1) * rows]
        store = pltpu.make_async_copy(buf.at[t], out.at[:, :, lanes], sem.at[t])
        store.start()
        stores.append(store)
    for store in stores:
        store.wait()


def solution(mesh):
    nf, nc = mesh.shape["facet"], mesh.shape["col"]

    def on_device(facets, observed, uv_cells, counts):
        rows, extent = facets.shape[1:]
        vis = observed.shape[2]
        pc = counts.shape[0]
        window = S // 8
        two = 2 * window
        groups = nf // 8
        wide = 2 - nc % 2
        assert pc == nf and nf % 8 == 0 and nf <= 32 and nc > wide
        constants = make_constants(nf, nc, pc, extent)
        vmem = pl.BlockSpec(memory_space=pltpu.VMEM)
        hbm = pl.BlockSpec(memory_space=pltpu.HBM)
        dma = pltpu.SemaphoreType.DMA
        fixed = functools.partial(pltpu.with_memory_space_constraint, memory_space=pltpu.HBM)
        back, base, tab = pl.pallas_call(
            functools.partial(cycle_kernel, nf, nc),
            out_shape=(
                jax.ShapeDtypeStruct((2 * nc - 2 * wide, window, rows), BF),
                jax.ShapeDtypeStruct((2 * rows, extent), F32),
                jax.ShapeDtypeStruct((nc * two, extent), BF),
            ),
            in_specs=[hbm] * 8,
            out_specs=(vmem, vmem, vmem),
            scratch_shapes=[
                pltpu.VMEM((2 * rows, extent), BF),
                pltpu.VMEM((2, pc, vis), F32),
                pltpu.VMEM((2, pc, vis), jnp.int32),
                pltpu.SMEM((pc,), jnp.int32),
                pltpu.VMEM((pc, 2, two), F32),
                pltpu.VMEM((nf, 2, two), F32),
                pltpu.VMEM((pc * two, extent), BF),
                pltpu.VMEM((extent, pc * two), BF),
                pltpu.VMEM((two, pc * two), F32),
                pltpu.VMEM((window, extent), F32),
                pltpu.VMEM((2, nc, window, rows), BF),
                pltpu.VMEM((2, nc, window, rows), BF),
                pltpu.VMEM((2, pc, window // 2, two), BF),
                pltpu.VMEM((2, nf, window // 2, two), BF),
                pltpu.VMEM((2 * S, vis), BF),
                pltpu.VMEM((vis, 2 * S), BF),
                pltpu.VMEM((S // 16, vis), F32),
                pltpu.VMEM((S // 16, vis), F32),
                pltpu.VMEM((2, groups * two, vis), F32),
                pltpu.VMEM((groups * two, vis), F32),
                pltpu.VMEM((groups * two, vis), BF),
                pltpu.VMEM((2, nf, window // 2, two), BF),
                pltpu.VMEM((2, pc, window // 2, two), BF),
                pltpu.VMEM((2, nc, window, rows), BF),
                pltpu.VMEM((2, nc, window, rows), BF),
                pltpu.SemaphoreType.REGULAR((2,)),
                dma((9,)), dma((nc // wide,)),
                dma((2,)), dma((2 * nc - 2,)), dma((2,)), dma((2, 2)),
                dma((2,)), dma((2, 2)), dma((2,)), dma((3,)),
            ],
            compiler_params=pltpu.CompilerParams(
                collective_id=0, has_side_effects=True, vmem_limit_bytes=44 * 2**20
            ),
            name="cycle",
        )(
            fixed(facets), fixed(observed), fixed(uv_cells), fixed(counts),
            *(fixed(jnp.asarray(constant)) for constant in constants),
        )
        tile = 256
        return pl.pallas_call(
            functools.partial(image_kernel, nc),
            out_shape=jax.ShapeDtypeStruct((2, rows, extent), F32),
            in_specs=[vmem, vmem, vmem],
            out_specs=hbm,
            scratch_shapes=[
                pltpu.VMEM((extent // tile, 2, rows, tile), F32),
                dma((extent // tile,)),
            ],
            compiler_params=pltpu.CompilerParams(vmem_limit_bytes=16 * 2**20),
            name="image",
        )(back, base, tab)

    return jax.shard_map(
        on_device,
        mesh=mesh,
        in_specs=(
            P(None, ("facet", "col"), None),
            P(None, "col", None),
            P(None, "col", None),
            P("col"),
        ),
        out_specs=P(None, ("facet", "col"), None),
        check_vma=False,
    )
```

time: 29.2 us -> 26.3 us (0.901)
  Pallas kernels: 29 us -> 26.2 us
    pallas_call x1, Pallas kernels: 27.2 us -> 24.5 us  [on_device(): pl.pallas_call(functools.partial(cycle_kernel, nf, nc), out_shape=(jax.Sh...]
where the time goes in v2:
time: 26.3 us; the launch traced here: 26.2 us
  Pallas kernels  26.2 us (100%)
    pallas_call x1, Pallas kernels, on_device(): pl.pallas_call(functools.partial(cycle_kernel, nf, nc), out_shape=(jax.Sh...  24.5 us
    pallas_call x1, Pallas kernels, on_device(): pl.pallas_call(functools.partial(image_kernel, nc), out_shape=jax.ShapeDt...  1.7 us

profile of v2, /device:TPU:0, one launch (start us, length us, event | category | flops | bytes accessed | tf_op | source)
XLA Modules:
  0.0 26.2 jit_solution(3534604556095620582)
XLA Ops:
  0.0 24.5 %cycle.1 = (bf16[4,64,256]{2,1,0:T(8,128)(2,1)S(1)}, f32[512,1024]{1,0:T(8,128)S(1)}, bf16[512,1024]{1,0:T(8,128)(2,1)S(1)}) custom-call(bf16[2,256,1024]{2,1,0:T(8,128)(2,1)} %x_hbm.1, f32[2,8,1024]{2,1,0:T(8,128)} %obs_hbm.1, s32[2,8,1024]{2,1,0:T(8,128)} %cells_hbm.1, s32[8]{0:T(128)} %counts_hbm.1, bf16[512,1024]{1,0:T(8,128)(2,1)} %constant.8.clone.ctab_hbm, ...), custom_call_target="tpu_custom_call" | custom-call | tf_op jit(solution)/shard_map/cycle/pallas_call | solution.py:502
  24.5 1.7 %image.1 = f32[2,256,1024]{2,1,0:T(8,128)} custom-call(bf16[4,64,256]{2,1,0:T(8,128)(2,1)S(1)} %get-tuple-element.8.back, f32[512,1024]{1,0:T(8,128)S(1)} %get-tuple-element.9.base, bf16[512,1024]{1,0:T(8,128)(2,1)S(1)} %get-tuple-element.10.tab), custom_call_target="tpu_custom_call" | custom-call | tf_op jit(solution)/shard_map/image/pallas_call | solution.py:551

commit v3 on v2

--- a/solution.py
+++ b/solution.py
@@ -133,11 +133,10 @@
     barrier = pltpu.get_barrier_semaphore()
     place, last_place = f // 2, nf // 2 - 1
     low, high = place > 0, place < last_place
+    far_low, far_high = place > 1, place < last_place - 1
 
     def signal(sem, facet, col):
         pl.semaphore_signal(sem, inc=1, device_id=(facet, col), device_id_type=MESH)
-
-    inside = low & high
 
     def pass_on(way):
         pl.semaphore_wait(tok.at[way], 1)
@@ -146,8 +145,17 @@
     for d in range(1, nc):
         signal(barrier, f, lax.rem(c + d, nc))
     signal(barrier, mate, c)
-    pl.when(high)(lambda: signal(barrier, f + 2, c))
-    pl.when(low)(lambda: signal(barrier, f - 2, c))
+
+    @pl.when(high)
+    def _():
+        signal(barrier, f + 2, c)
+        signal(barrier, mate + 2, c)
+
+    @pl.when(low)
+    def _():
+        signal(barrier, f - 2, c)
+        signal(barrier, mate - 2, c)
+
 
     n_groups = nc // wide
     chunk = wide * window
@@ -157,52 +165,48 @@
 
     far_groups = list(range(n_groups - 1, 0, -1)) if wide == 2 else list(range(1, nc))
 
-    def tab_load(d):
+    def tab_load(d, lanes, sem):
         at = pl.ds(pl.multiple_of(group_at(d) * 2 * chunk, 2 * chunk), 2 * chunk)
-        return pltpu.make_async_copy(ctab_hbm.at[at], tab.at[at], tab_sem.at[d])
-
-    x_loads = [
-        pltpu.make_async_copy(x_hbm.at[k], xbuf.at[k * rows : (k + 1) * rows], in_sem.at[k])
-        for k in range(2)
+        return pltpu.make_async_copy(ctab_hbm.at[at, lanes], tab.at[at, lanes], sem)
+
+    depth = xbuf.shape[1] // 2
+    depths = [slice(k * depth, (k + 1) * depth) for k in range(2)]
+    early = [
+        [tab_load(d, lanes, tab_sem.at[k, d]) for d in far_groups]
+        + [
+            pltpu.make_async_copy(
+                x_hbm.at[p, :, lanes], xbuf.at[p * rows : (p + 1) * rows, lanes], in_sem.at[2 * k + p]
+            )
+            for p in range(2)
+        ]
+        for k, lanes in enumerate(depths)
     ]
-    row_load = pltpu.make_async_copy(rtab_hbm, t2, in_sem.at[2])
+    mine_load = tab_load(0, slice(None), tab_sem.at[0, 0])
+    row_load = pltpu.make_async_copy(rtab_hbm, t2, in_sem.at[9])
     small_loads = [
-        pltpu.make_async_copy(turn_hbm.at[f, c], turn_in, in_sem.at[3]),
-        pltpu.make_async_copy(turn_hbm.at[:, c, f], turn_out, in_sem.at[4]),
-        pltpu.make_async_copy(obs_hbm, obs, in_sem.at[5]),
-        pltpu.make_async_copy(cells_hbm, cells, in_sem.at[6]),
-        pltpu.make_async_copy(counts_hbm, counts, in_sem.at[7]),
+        pltpu.make_async_copy(turn_hbm.at[f, c], turn_in, in_sem.at[4]),
+        pltpu.make_async_copy(turn_hbm.at[:, c, f], turn_out, in_sem.at[5]),
+        pltpu.make_async_copy(obs_hbm, obs, in_sem.at[6]),
+        pltpu.make_async_copy(cells_hbm, cells, in_sem.at[7]),
+        pltpu.make_async_copy(counts_hbm, counts, in_sem.at[8]),
     ]
-    turned_load = pltpu.make_async_copy(ttab_hbm, tt, in_sem.at[8])
-    for n, d in enumerate(far_groups + [0]):
-        tab_load(d).start()
-        if n == 0:
-            for load in x_loads:
-                load.start()
-    for load in small_loads:
+    turned_load = pltpu.make_async_copy(ttab_hbm, tt, in_sem.at[10])
+    for load in early[0] + early[1]:
         load.start()
 
-    pl.semaphore_wait(barrier, nc + low.astype(jnp.int32) + high.astype(jnp.int32))
-    pl.when(~low)(lambda: signal(tok.at[0], f + 2, c))
-    pl.when(~high)(lambda: signal(tok.at[1], f - 2, c))
-
-    for load in x_loads:
-        load.wait()
-    turned_load.start()
-
-    def strips(d, first_part, n_parts):
-        at = pl.multiple_of(group_at(d) * 2 * chunk + first_part * chunk, chunk)
-        both = lax.dot_general(
-            tab[pl.ds(at, n_parts * chunk), :], xbuf[...], NT, preferred_element_type=F32
+    def strip_term(d, lanes):
+        at = pl.multiple_of(group_at(d) * 2 * chunk, 2 * chunk)
+        return lax.dot_general(
+            tab[pl.ds(at, 2 * chunk), lanes], xbuf[:, lanes], NT, preferred_element_type=F32
         )
-        for part in range(n_parts):
+
+    def strips(d, both):
+        for part in range(2):
             for k in range(wide):
                 at = part * chunk + k * window
                 real, imag = both[at : at + half], both[at + half : at + window]
                 block = [real[:, :rows] - imag[:, rows:], imag[:, :rows] + real[:, rows:]]
-                s_send[first_part + part, wide * group_at(d) + k] = jnp.concatenate(
-                    block, axis=0
-                ).astype(BF)
+                s_send[part, wide * group_at(d) + k] = jnp.concatenate(block, axis=0).astype(BF)
 
     def send_strips(d, part):
         for n, step in enumerate(col_steps):
@@ -210,18 +214,35 @@
                 at = part * len(col_steps) + n
                 col_link(s_send, s_recv, sa, ra.at[at], part, col_at(step, 1), c).start()
 
-    for n, d in enumerate(far_groups):
-        tab_load(d).wait()
+    for load in early[0]:
+        load.wait()
+    mine_load.start()
+    for load in small_loads:
+        load.start()
+    sums = [strip_term(d, depths[0]) for d in far_groups]
+    for load in early[1]:
+        load.wait()
+    turned_load.start()
+    for d, term in zip(far_groups, sums):
+        strips(d, term + strip_term(d, depths[1]))
+    pl.semaphore_wait(barrier, nc + 2 * low.astype(jnp.int32) + 2 * high.astype(jnp.int32))
     for part in range(2):
         for d in far_groups:
-            strips(d, part, 1)
             send_strips(d, part)
-    pl.when(inside & (place == last_place - 1))(functools.partial(pass_on, 1))
-    tab_load(0).wait()
-    strips(0, 0, 2)
+    pl.when((place == 1) & high)(lambda: signal(tok.at[0], f + 2, c))
+    pl.when((place == last_place - 1) & low)(lambda: signal(tok.at[1], f - 2, c))
+    mine_load.wait()
+    strips(0, strip_term(0, slice(None)))
     for part in range(2):
         send_strips(0, part)
-    pl.when(inside & (place == 1))(functools.partial(pass_on, 0))
+
+    @pl.when(far_low & high)
+    def _():
+        pass_on(0)
+
+    @pl.when(far_high & low)
+    def _():
+        pass_on(1)
 
     turned_load.wait()
 
@@ -230,8 +251,6 @@
         return jnp.dot(block, tt[pl.ds(at, rows), :], preferred_element_type=F32)
 
     acc[...] = window_term(jnp.concatenate([s_send[0, c], s_send[1, c]], axis=0), c)
-    pl.when(inside & (place != 1))(functools.partial(pass_on, 0))
-    pl.when(inside & (place != last_place - 1))(functools.partial(pass_on, 1))
 
     for load in small_loads:
         load.wait()
@@ -290,11 +309,9 @@
             win += pltpu.roll(u, window, 1) * cross + v * sign(cross, 1.0, -1.0)
             g_send[part, j] = win.astype(BF)
         if part == 0:
-            pl.when(~low)(lambda: pl.semaphore_wait(tok.at[1], 1))
-            pl.when(~high)(lambda: pl.semaphore_wait(tok.at[0], 1))
+            pl.when(far_high & ~low)(lambda: pl.semaphore_wait(tok.at[1], 1))
+            pl.when(far_low & ~high)(lambda: pl.semaphore_wait(tok.at[0], 1))
         send_facets(g_send, g_recv, sb, rb, part)
-
-    windows(0)
 
     first = cells[0, pl.ds(f, 1), :]
     second = cells[1, pl.ds(f, 1), :]
@@ -319,6 +336,8 @@
     m0r, m0i = wave(16, 1, second)
     m0r, m0i = m0r * gain, m0i * gain
     r1r[...], r1i[...] = wave(S // 16, 16, second)
+
+    windows(0)
 
     def right_body(i, carry):
         er, ei = r1r[pl.ds(i, 1), :], r1i[pl.ds(i, 1), :]
@@ -535,7 +554,7 @@
                 pltpu.VMEM((2, nc, window, rows), BF),
                 pltpu.VMEM((2, nc, window, rows), BF),
                 pltpu.SemaphoreType.REGULAR((2,)),
-                dma((9,)), dma((nc // wide,)),
+                dma((11,)), dma((2, nc // wide)),
                 dma((2,)), dma((2 * nc - 2,)), dma((2,)), dma((2, 2)),
                 dma((2,)), dma((2, 2)), dma((2,)), dma((3,)),
             ],

time: 26.3 us -> 25.3 us (0.962)
  Pallas kernels: 26.2 us -> 25.2 us
    pallas_call x1, Pallas kernels: 24.5 us -> 23.5 us  [on_device(): pl.pallas_call(functools.partial(cycle_kernel, nf, nc), out_shape=(jax.Sh...]
where the time goes in v3:
time: 25.3 us; the launch traced here: 25.2 us
  Pallas kernels  25.2 us (100%)
    pallas_call x1, Pallas kernels, on_device(): pl.pallas_call(functools.partial(cycle_kernel, nf, nc), out_shape=(jax.Sh...  23.5 us
    pallas_call x1, Pallas kernels, on_device(): pl.pallas_call(functools.partial(image_kernel, nc), out_shape=jax.ShapeDt...  1.7 us

profile of v3, /device:TPU:0, one launch (start us, length us, event | category | flops | bytes accessed | tf_op | source)
XLA Modules:
  0.0 25.2 jit_solution(13157244839142452994)
XLA Ops:
  0.0 23.5 %cycle.1 = (bf16[4,64,256]{2,1,0:T(8,128)(2,1)S(1)}, f32[512,1024]{1,0:T(8,128)S(1)}, bf16[512,1024]{1,0:T(8,128)(2,1)S(1)}) custom-call(bf16[2,256,1024]{2,1,0:T(8,128)(2,1)} %x_hbm.1, f32[2,8,1024]{2,1,0:T(8,128)} %obs_hbm.1, s32[2,8,1024]{2,1,0:T(8,128)} %cells_hbm.1, s32[8]{0:T(128)} %counts_hbm.1, bf16[512,1024]{1,0:T(8,128)(2,1)} %constant.8.clone.ctab_hbm, ...), custom_call_target="tpu_custom_call" | custom-call | tf_op jit(solution)/shard_map/cycle/pallas_call | solution.py:521
  23.5 1.7 %image.1 = f32[2,256,1024]{2,1,0:T(8,128)} custom-call(bf16[4,64,256]{2,1,0:T(8,128)(2,1)S(1)} %get-tuple-element.8.back, f32[512,1024]{1,0:T(8,128)S(1)} %get-tuple-element.9.base, bf16[512,1024]{1,0:T(8,128)(2,1)S(1)} %get-tuple-element.10.tab), custom_call_target="tpu_custom_call" | custom-call | tf_op jit(solution)/shard_map/image/pallas_call | solution.py:570

commit v4 on v3

--- a/solution.py
+++ b/solution.py
@@ -112,19 +112,16 @@
     def group_of(q):
         return 0 if q in waits[0] else 1
 
-    def facet_link(src_buf, dst_buf, send, recv, part, peer, slot, group):
+    def facet_link(src_buf, dst_buf, send, recv, part, peer):
         return pltpu.make_async_remote_copy(
-            src_buf.at[part, peer], dst_buf.at[part, slot],
-            send.at[part], recv.at[part, group], (peer, c), MESH,
+            src_buf.at[part * nf + peer], dst_buf.at[part * nf + f], send, recv, (peer, c), MESH
         )
 
-    def col_link(src_buf, dst_buf, send, recv, part, peer, slot):
-        return pltpu.make_async_remote_copy(
-            src_buf.at[part, peer], dst_buf.at[part, slot], send.at[part], recv, (f, peer), MESH
-        )
-
-    def sum_of(buf, part, count, send, recv):
-        some = buf.at[part, 0:count]
+    def col_link(src, dst, send, recv, peer):
+        return pltpu.make_async_remote_copy(src, dst, send, recv, (f, peer), MESH)
+
+    def sum_of(buf, start, count, send, recv):
+        some = buf.at[start : start + count]
         return pltpu.make_async_remote_copy(some, some, send, recv, (mate, c), MESH)
 
     waits = ((0, 1), (3, 2))
@@ -149,12 +146,12 @@
     @pl.when(high)
     def _():
         signal(barrier, f + 2, c)
-        signal(barrier, mate + 2, c)
+        pl.when(~low)(lambda: signal(barrier, mate + 2, c))
 
     @pl.when(low)
     def _():
         signal(barrier, f - 2, c)
-        signal(barrier, mate - 2, c)
+        pl.when(~high)(lambda: signal(barrier, mate - 2, c))
 
 
     n_groups = nc // wide
@@ -169,8 +166,8 @@
         at = pl.ds(pl.multiple_of(group_at(d) * 2 * chunk, 2 * chunk), 2 * chunk)
         return pltpu.make_async_copy(ctab_hbm.at[at, lanes], tab.at[at, lanes], sem)
 
-    depth = xbuf.shape[1] // 2
-    depths = [slice(k * depth, (k + 1) * depth) for k in range(2)]
+    quarter = xbuf.shape[1] // 4
+    depths = [slice(0, quarter), slice(quarter, 2 * quarter), slice(2 * quarter, 4 * quarter)]
     early = [
         [tab_load(d, lanes, tab_sem.at[k, d]) for d in far_groups]
         + [
@@ -182,16 +179,16 @@
         for k, lanes in enumerate(depths)
     ]
     mine_load = tab_load(0, slice(None), tab_sem.at[0, 0])
-    row_load = pltpu.make_async_copy(rtab_hbm, t2, in_sem.at[9])
+    row_load = pltpu.make_async_copy(rtab_hbm, t2, in_sem.at[13])
     small_loads = [
-        pltpu.make_async_copy(turn_hbm.at[f, c], turn_in, in_sem.at[4]),
-        pltpu.make_async_copy(turn_hbm.at[:, c, f], turn_out, in_sem.at[5]),
-        pltpu.make_async_copy(obs_hbm, obs, in_sem.at[6]),
-        pltpu.make_async_copy(cells_hbm, cells, in_sem.at[7]),
-        pltpu.make_async_copy(counts_hbm, counts, in_sem.at[8]),
+        pltpu.make_async_copy(turn_hbm.at[f, c], turn_in, in_sem.at[8]),
+        pltpu.make_async_copy(turn_hbm.at[:, c, f], turn_out, in_sem.at[9]),
+        pltpu.make_async_copy(obs_hbm, obs, in_sem.at[10]),
+        pltpu.make_async_copy(cells_hbm, cells, in_sem.at[11]),
+        pltpu.make_async_copy(counts_hbm, counts, in_sem.at[12]),
     ]
-    turned_load = pltpu.make_async_copy(ttab_hbm, tt, in_sem.at[10])
-    for load in early[0] + early[1]:
+    turned_load = pltpu.make_async_copy(ttab_hbm, tt, in_sem.at[14])
+    for load in sum(early, []):
         load.start()
 
     def strip_term(d, lanes):
@@ -201,40 +198,48 @@
         )
 
     def strips(d, both):
-        for part in range(2):
-            for k in range(wide):
-                at = part * chunk + k * window
-                real, imag = both[at : at + half], both[at + half : at + window]
+        for k in range(wide):
+            for part in range(parts):
+                at = part // 2 * chunk + k * window + part % 2 * 16
+                real, imag = both[at : at + 16], both[at + half : at + half + 16]
                 block = [real[:, :rows] - imag[:, rows:], imag[:, :rows] + real[:, rows:]]
-                s_send[part, wide * group_at(d) + k] = jnp.concatenate(block, axis=0).astype(BF)
-
-    def send_strips(d, part):
-        for n, step in enumerate(col_steps):
-            if step[0] == d:
-                at = part * len(col_steps) + n
-                col_link(s_send, s_recv, sa, ra.at[at], part, col_at(step, 1), c).start()
-
-    for load in early[0]:
-        load.wait()
-    mine_load.start()
-    for load in small_loads:
-        load.start()
-    sums = [strip_term(d, depths[0]) for d in far_groups]
-    for load in early[1]:
-        load.wait()
-    turned_load.start()
-    for d, term in zip(far_groups, sums):
-        strips(d, term + strip_term(d, depths[1]))
-    pl.semaphore_wait(barrier, nc + 2 * low.astype(jnp.int32) + 2 * high.astype(jnp.int32))
-    for part in range(2):
-        for d in far_groups:
-            send_strips(d, part)
+                s_send[wide * group_at(d) + k, part] = jnp.concatenate(block, axis=0).astype(BF)
+
+    def strip_link(step, part):
+        peer = col_at(step, 1)
+        at = ra.at[part * len(far_steps) + far_steps.index(step)]
+        return col_link(s_send.at[peer, part], s_recv.at[c, part], sa.at[0], at, peer)
+
+    def near_link(step):
+        peer = col_at(step, 1)
+        at = ra.at[parts * len(far_steps) + near_steps.index(step)]
+        return col_link(s_send.at[peer], s_recv.at[c], sa.at[0], at, peer)
+
+    sums = [0.0] * len(far_groups)
+    for lanes, loads in zip(depths, early):
+        for load in loads:
+            load.wait()
+        if lanes is depths[0]:
+            mine_load.start()
+            for load in small_loads:
+                load.start()
+        if lanes is depths[-1]:
+            turned_load.start()
+        for n, d in enumerate(far_groups):
+            sums[n] += strip_term(d, lanes)
+    for d, both in zip(far_groups, sums):
+        strips(d, both)
+    greeted = (low, high, place == 1, place == last_place - 1)
+    pl.semaphore_wait(barrier, nc + sum(one.astype(jnp.int32) for one in greeted))
+    for part in range(parts):
+        for step in far_steps:
+            strip_link(step, part).start()
     pl.when((place == 1) & high)(lambda: signal(tok.at[0], f + 2, c))
     pl.when((place == last_place - 1) & low)(lambda: signal(tok.at[1], f - 2, c))
     mine_load.wait()
     strips(0, strip_term(0, slice(None)))
-    for part in range(2):
-        send_strips(0, part)
+    for step in near_steps:
+        near_link(step).start()
 
     @pl.when(far_low & high)
     def _():
@@ -250,68 +255,18 @@
         at = pl.multiple_of(src * rows, rows)
         return jnp.dot(block, tt[pl.ds(at, rows), :], preferred_element_type=F32)
 
-    acc[...] = window_term(jnp.concatenate([s_send[0, c], s_send[1, c]], axis=0), c)
+    acc[...] = window_term(s_send[c].reshape(two, rows), c)
 
     for load in small_loads:
         load.wait()
 
-    def each_facet(q, act):
-        pair = pair_at(q)
-        for g in range(groups):
-            for h in range(2):
-                index = g * 8 + 2 * pair + h
-                if q == 0:
-                    pl.when(index != f)(functools.partial(act, index))
-                else:
-                    act(index)
-
-    def send_facets(src_buf, dst_buf, send, recv, part):
-        for q in far_first:
-            each_facet(
-                q,
-                lambda index, q=q: facet_link(
-                    src_buf, dst_buf, send, recv, part, index, f, group_of(-q % 4)
-                ).start(),
-            )
-        dst_buf[part, f] = src_buf[part, f]
-
-    def take_facets(buf, send, recv, part, pairs):
-        for group in range(2):
-            if waits[group][0] in pairs:
-                count = 4 * groups - (0 in waits[group])
-                sum_of(buf, part, count, send.at[part], recv.at[part, group]).wait_recv()
-
-    far_first = (2, 3, 1, 0)
-
-    def take_strip(part, step):
-        src = col_at(step, -1)
-        at = part * len(col_steps) + col_steps.index(step)
-        col_link(s_send, s_recv, sa, ra.at[at], part, src, src).wait_recv()
-
-    for step in near_steps:
-        src = col_at(step, -1)
-        for part in range(2):
-            take_strip(part, step)
-        acc[...] += window_term(jnp.concatenate([s_recv[0, src], s_recv[1, src]], axis=0), src)
-
-    def windows(part):
-        total = acc[part * window : (part + 1) * window]
-        for step in far_steps:
-            src = col_at(step, -1)
-            take_strip(part, step)
-            total += window_term(s_recv[part, src], src)
-        for j in range(pc):
-            u = total[:half, j * two : (j + 1) * two]
-            v = total[half:, j * two : (j + 1) * two]
-            turn = turn_in[j]
-            same, cross = turn[0:1], turn[1:2]
-            win = u * same + spin(v, -1.0, 1.0) * same
-            win += pltpu.roll(u, window, 1) * cross + v * sign(cross, 1.0, -1.0)
-            g_send[part, j] = win.astype(BF)
-        if part == 0:
-            pl.when(far_high & ~low)(lambda: pl.semaphore_wait(tok.at[1], 1))
-            pl.when(far_low & ~high)(lambda: pl.semaphore_wait(tok.at[0], 1))
-        send_facets(g_send, g_recv, sb, rb, part)
+    def send_windows(part):
+        def act(index):
+            facet_link(g_send, g_recv, sb.at[0], rb.at[part], part, index).start()
+
+        for index in range(nf - 1, -1, -1):
+            pl.when(index != f)(functools.partial(act, index))
+        g_recv[part * nf + f] = g_send[part * nf + f]
 
     first = cells[0, pl.ds(f, 1), :]
     second = cells[1, pl.ds(f, 1), :]
@@ -337,29 +292,52 @@
     m0r, m0i = m0r * gain, m0i * gain
     r1r[...], r1i[...] = wave(S // 16, 16, second)
 
-    windows(0)
-
     def right_body(i, carry):
         er, ei = r1r[pl.ds(i, 1), :], r1i[pl.ds(i, 1), :]
         b = i // parts
         k = i - b * parts
-        h = k // (parts // 2)
-        at = pl.multiple_of(h * S + b * window + (k - h * (parts // 2)) * 16, 16)
+        at = pl.multiple_of(k * (2 * S // parts) + b * half, 16)
         right[pl.ds(at, 16), :] = (m0r * er - m0i * ei).astype(BF)
-        right[pl.ds(at + half, 16), :] = (m0r * ei + m0i * er).astype(BF)
+        right[pl.ds(at + 16, 16), :] = (m0r * ei + m0i * er).astype(BF)
         return carry
 
     lax.fori_loop(0, S // 16, right_body, 0)
 
-    windows(1)
+    for step in near_steps:
+        near_link(step).wait_recv()
+        src = col_at(step, -1)
+        acc[...] += window_term(s_recv[src].reshape(two, rows), src)
+
+    def windows(some):
+        lo, hi = some[0], some[-1] + 1
+        total = acc[lo * half : hi * half]
+        for step in far_steps:
+            for part in some:
+                strip_link(step, part).wait_recv()
+            src = col_at(step, -1)
+            block = s_recv[src, lo:hi].reshape((hi - lo) * half, rows)
+            total += window_term(block, src)
+        for part in some:
+            at = (part - lo) * half
+            for j in range(pc):
+                u = total[at : at + 16, j * two : (j + 1) * two]
+                v = total[at + 16 : at + half, j * two : (j + 1) * two]
+                turn = turn_in[j]
+                same, cross = turn[0:1], turn[1:2]
+                win = u * same + spin(v, -1.0, 1.0) * same
+                win += pltpu.roll(u, window, 1) * cross + v * sign(cross, 1.0, -1.0)
+                g_send[part * pc + j] = win.astype(BF)
+        if 0 in some:
+            pl.when(far_high & ~low)(lambda: pl.semaphore_wait(tok.at[1], 1))
+            pl.when(far_low & ~high)(lambda: pl.semaphore_wait(tok.at[0], 1))
+        for part in some:
+            send_windows(part)
+
+    windows([0])
+
+    windows([1])
+    windows(list(range(2, parts)))
     row_load.start()
-
-    def turn_body(i, carry):
-        at = pl.multiple_of(i * two, two)
-        right_t[:, pl.ds(at, two)] = right[pl.ds(at, two), :].T
-        return carry
-
-    lax.fori_loop(0, S // window, turn_body, 0)
 
     l0r, l0i = wave(16, 1, first)
     l1r, l1i = wave(max(groups * parts, 8), 16, first)
@@ -373,65 +351,96 @@
         left[1, at : at + 16, :] = imag
         left[1, at + window : at + window + 16, :] = real
 
-    def pred_term(part, pairs, g):
-        blocks, tables = [], []
-        for q in pairs:
-            for h in range(2):
-                block = g_recv[part, g * 8 + 2 * pair_at(q) + h].astype(F32)
+    deep = 2 * S // parts
+
+    def turn_body(b, carry):
+        pieces = [right[pl.ds(pl.multiple_of(k * deep + b * half, 16), half), :] for k in range(parts)]
+        at = pl.multiple_of(b * two, two)
+        right_t[:, pl.ds(at, two)] = jnp.concatenate(pieces, axis=0).T
+        return carry
+
+    lax.fori_loop(0, S // window, turn_body, 0)
+
+    def pred_term(some, g):
+        blocks = []
+        for part in some:
+            for b in range(8):
+                block = g_recv[part * nf + g * 8 + b].astype(F32)
                 blocks += [block, spin(block, -1.0, 1.0)]
-            at = pl.multiple_of(part * S + pair_at(q) * two, two)
-            tables.append(right[pl.ds(at, two), :])
         return jnp.dot(
             jnp.concatenate(blocks, axis=0).T.astype(BF),
-            jnp.concatenate(tables, axis=0),
+            right[some[0] * deep : (some[-1] + 1) * deep, :],
             preferred_element_type=F32,
         )
 
-    for part in range(2):
-        for pairs in waits if part else (waits[0] + waits[1],):
-            take_facets(g_recv, sb, rb, part, pairs)
-            if pairs == waits[1]:
-                continue
-            for g in range(groups):
-                at = slice(g * two, (g + 1) * two)
-                if part == 0:
-                    inner[at] = pred_term(part, pairs, g)
-                else:
-                    inner[at] += pred_term(part, pairs, g)
+    def take_windows(some):
+        for part in some:
+            sum_of(g_recv, part * nf, nf - 1, sb.at[0], rb.at[part]).wait_recv()
+
+    early_parts, late_parts = list(range(parts // 2)), list(range(parts // 2, parts))
+    take_windows(early_parts)
+    for g in range(groups):
+        inner[g * two : (g + 1) * two] = pred_term(early_parts, g)
+
+    for part in late_parts[:-1]:
+        take_windows([part])
+        for g in range(groups):
+            inner[g * two : (g + 1) * two] += pred_term([part], g)
+    take_windows(late_parts[-1:])
     res_r, res_i = obs[0, pl.ds(f, 1), :], obs[1, pl.ds(f, 1), :]
     for g in range(groups):
         at = slice(g * two, (g + 1) * two)
-        value = inner[at] + pred_term(1, waits[-1], g)
+        value = inner[at] + pred_term(late_parts[-1:], g)
         unscale = 1.0 / (scale * S)
         res_r -= jnp.sum(value * left[0, at], axis=0, keepdims=True) * unscale
         res_i -= jnp.sum(value * left[1, at], axis=0, keepdims=True) * unscale
     held[...] = (res_r * left[0] + res_i * left[1]).astype(BF)
 
-    for part in range(2):
-        grid = jnp.dot(
-            held[...], right_t[:, part * S : (part + 1) * S], preferred_element_type=F32
-        )
+    def send_back(part, index):
+        def act(group):
+            recv = rc.at[2 * part + group]
+            facet_link(r_send, r_recv, sc.at[0], recv, part, index).start()
+
+        near = lax.rem(place - index // 2 + nf // 2, 4)
+        pl.when((near < 2) & (index != f))(lambda: act(0))
+        pl.when(near >= 2)(lambda: act(1))
+
+    def grid_blocks(lo, hi):
+        grid = jnp.dot(held[...], right_t[:, lo * two : hi * two], preferred_element_type=F32)
         for g in range(groups):
             block_t = grid[g * two : (g + 1) * two].T
-            for b in range(8):
-                u = block_t[b * window : b * window + half]
-                v = block_t[b * window + half : (b + 1) * window]
+            for b in range(lo, hi):
                 turn = turn_out[g * 8 + b]
                 same, cross = turn[0:1], turn[1:2]
-                block = (u + spin(v, 1.0, -1.0)) * same
-                block -= pltpu.roll(u, window, 1) * cross + v * sign(cross, -1.0, 1.0)
-                r_send[part, g * 8 + b] = block.astype(BF)
-        send_facets(r_send, r_recv, sc, rc, part)
+                for part in range(2):
+                    starts = [(b - lo) * two + (2 * part + k) * half for k in range(2)]
+                    u = jnp.concatenate([block_t[at : at + 16] for at in starts], axis=0)
+                    v = jnp.concatenate([block_t[at + 16 : at + half] for at in starts], axis=0)
+                    block = (u + spin(v, 1.0, -1.0)) * same
+                    block -= pltpu.roll(u, window, 1) * cross + v * sign(cross, -1.0, 1.0)
+                    r_send[part * nf + g * 8 + b] = block.astype(BF)
+
+    grid_blocks(0, 2)
+    for part in range(2):
+        for index in range(2):
+            send_back(part, index)
+    grid_blocks(2, 8)
+    for part in range(2):
+        for index in range(2, nf):
+            send_back(part, index)
+        r_recv[part * nf + f] = r_send[part * nf + f]
 
     row_load.wait()
 
     def back_term(part, pairs):
         total = None
-        take_facets(r_recv, sc, rc, part, pairs)
+        group = waits.index(pairs)
+        count = 4 * groups - (0 in pairs)
+        sum_of(r_recv, part * nf, count, sc.at[0], rc.at[2 * part + group]).wait_recv()
         for q in pairs:
             for g in range(groups):
                 first = g * 8 + 2 * pair_at(q)
-                pieces = [r_recv[part, first + h] for h in range(2)]
+                pieces = [r_recv[part * nf + first + h] for h in range(2)]
                 spun = [spin(piece.astype(F32), 1.0, -1.0).astype(BF) for piece in pieces]
                 block = jnp.concatenate(
                     [jnp.concatenate(pieces, axis=1), jnp.concatenate(spun, axis=1)], axis=0
@@ -444,11 +453,14 @@
     def back_strips(part):
         total = (bacc[...] + back_term(part, waits[1])).astype(BF)
         for cp in range(nc):
-            b_send[part, cp] = total[:, cp * rows : (cp + 1) * rows]
+            b_send[part * nc + cp] = total[:, cp * rows : (cp + 1) * rows]
         for step in col_steps:
+            peer = col_at(step, 1)
             at = rd.at[0 if step in near_steps else 1 + part]
-            col_link(b_send, b_recv, sd, at, part, col_at(step, 1), c).start()
-        b_recv[part, c] = b_send[part, c]
+            col_link(
+                b_send.at[part * nc + peer], b_recv.at[part * nc + c], sd.at[0], at, peer
+            ).start()
+        b_recv[part * nc + c] = b_send[part * nc + c]
 
     bacc[...] = back_term(0, waits[0])
     back_strips(0)
@@ -456,22 +468,21 @@
     back_strips(1)
     if near_steps:
         sum_of(b_recv, 0, 2 * len(near_steps), sd.at[0], rd.at[0]).wait_recv()
-    mine = [b_recv[part, wide * group_at(0) + k] for part in range(2) for k in range(wide)]
+    mine = [b_recv[part * nc + wide * group_at(0) + k] for part in range(2) for k in range(wide)]
     at = pl.multiple_of(group_at(0) * 2 * chunk, 2 * chunk)
     base_out[...] = jnp.dot(
         image_rows(mine), tab[pl.ds(at, 2 * chunk), :], preferred_element_type=F32
     )
-    sum_of(b_recv, 0, len(far_steps), sd.at[0], rd.at[1]).wait_recv()
-    sum_of(b_recv, 1, len(far_steps), sd.at[1], rd.at[2]).wait_recv()
     for part in range(2):
+        sum_of(b_recv, 0, len(far_steps), sd.at[0], rd.at[1 + part]).wait_recv()
         for d in range(1, n_groups):
             for k in range(wide):
-                back_out[((d - 1) * 2 + part) * wide + k] = b_recv[part, wide * group_at(d) + k]
-    for part in range(2):
-        sum_of(s_send, part, nc - 1, sa.at[part], rd.at[0]).wait_send()
-        sum_of(b_send, part, nc - 1, sd.at[part], rd.at[0]).wait_send()
-        sum_of(g_send, part, nf - 1, sb.at[part], rb.at[0, 0]).wait_send()
-        sum_of(r_send, part, nf - 1, sc.at[part], rc.at[0, 0]).wait_send()
+                at = part * nc + wide * group_at(d) + k
+                back_out[((d - 1) * 2 + part) * wide + k] = b_recv[at]
+    sum_of(s_send, 0, nc - 1, sa.at[0], ra.at[0]).wait_send()
+    sum_of(b_send, 0, 2 * (nc - 1), sd.at[0], rd.at[0]).wait_send()
+    sum_of(g_send, 0, parts * (nf - 1), sb.at[0], rb.at[0]).wait_send()
+    sum_of(r_send, 0, 2 * (nf - 1), sc.at[0], rc.at[0]).wait_send()
 
 
 def image_kernel(nc, back, base, tab, out, buf, sem):
@@ -512,6 +523,7 @@
         two = 2 * window
         groups = nf // 8
         wide = 2 - nc % 2
+        parts = window // 16
         assert pc == nf and nf % 8 == 0 and nf <= 32 and nc > wide
         constants = make_constants(nf, nc, pc, extent)
         vmem = pl.BlockSpec(memory_space=pltpu.VMEM)
@@ -538,10 +550,10 @@
                 pltpu.VMEM((extent, pc * two), BF),
                 pltpu.VMEM((two, pc * two), F32),
                 pltpu.VMEM((window, extent), F32),
-                pltpu.VMEM((2, nc, window, rows), BF),
-                pltpu.VMEM((2, nc, window, rows), BF),
-                pltpu.VMEM((2, pc, window // 2, two), BF),
-                pltpu.VMEM((2, nf, window // 2, two), BF),
+                pltpu.VMEM((nc, parts, window // 2, rows), BF),
+                pltpu.VMEM((nc, parts, window // 2, rows), BF),
+                pltpu.VMEM((parts * pc, 16, two), BF),
+                pltpu.VMEM((parts * nf, 16, two), BF),
                 pltpu.VMEM((2 * S, vis), BF),
                 pltpu.VMEM((vis, 2 * S), BF),
                 pltpu.VMEM((S // 16, vis), F32),
@@ -549,14 +561,14 @@
                 pltpu.VMEM((2, groups * two, vis), F32),
                 pltpu.VMEM((groups * two, vis), F32),
                 pltpu.VMEM((groups * two, vis), BF),
-                pltpu.VMEM((2, nf, window // 2, two), BF),
-                pltpu.VMEM((2, pc, window // 2, two), BF),
-                pltpu.VMEM((2, nc, window, rows), BF),
-                pltpu.VMEM((2, nc, window, rows), BF),
+                pltpu.VMEM((2 * nf, window // 2, two), BF),
+                pltpu.VMEM((2 * pc, window // 2, two), BF),
+                pltpu.VMEM((2 * nc, window, rows), BF),
+                pltpu.VMEM((2 * nc, window, rows), BF),
                 pltpu.SemaphoreType.REGULAR((2,)),
-                dma((11,)), dma((2, nc // wide)),
-                dma((2,)), dma((2 * nc - 2,)), dma((2,)), dma((2, 2)),
-                dma((2,)), dma((2, 2)), dma((2,)), dma((3,)),
+                dma((15,)), dma((4, nc // wide)),
+                dma((1,)), dma((parts * (nc - wide) + wide - 1,)), dma((1,)), dma((parts,)),
+                dma((1,)), dma((4,)), dma((1,)), dma((3,)),
             ],
             compiler_params=pltpu.CompilerParams(
                 collective_id=0, has_side_effects=True, vmem_limit_bytes=44 * 2**20

time: 25.3 us -> 24.6 us (0.972)
  Pallas kernels: 25.2 us -> 24.4 us
    pallas_call x1, Pallas kernels: 23.5 us -> 22.7 us  [on_device(): pl.pallas_call(functools.partial(cycle_kernel, nf, nc), out_shape=(jax.Sh...]
where the time goes in v4:
time: 24.6 us; the launch traced here: 24.4 us
  Pallas kernels  24.4 us (99%)
    pallas_call x1, Pallas kernels, on_device(): pl.pallas_call(functools.partial(cycle_kernel, nf, nc), out_shape=(jax.Sh...  22.7 us
    pallas_call x1, Pallas kernels, on_device(): pl.pallas_call(functools.partial(image_kernel, nc), out_shape=jax.ShapeDt...  1.7 us

profile of v4, /device:TPU:0, one launch (start us, length us, event | category | flops | bytes accessed | tf_op | source)
XLA Modules:
  0.0 24.4 jit_solution(11907380534724617773)
XLA Ops:
  0.0 22.7 %cycle.1 = (bf16[4,64,256]{2,1,0:T(8,128)(2,1)S(1)}, f32[512,1024]{1,0:T(8,128)S(1)}, bf16[512,1024]{1,0:T(8,128)(2,1)S(1)}) custom-call(bf16[2,256,1024]{2,1,0:T(8,128)(2,1)} %x_hbm.1, f32[2,8,1024]{2,1,0:T(8,128)} %obs_hbm.1, s32[2,8,1024]{2,1,0:T(8,128)} %cells_hbm.1, s32[8]{0:T(128)} %counts_hbm.1, bf16[512,1024]{1,0:T(8,128)(2,1)} %constant.8.clone.ctab_hbm, ...), custom_call_target="tpu_custom_call" | custom-call | tf_op jit(solution)/shard_map/cycle/pallas_call | solution.py:533
  22.7 1.7 %image.1 = f32[2,256,1024]{2,1,0:T(8,128)} custom-call(bf16[4,64,256]{2,1,0:T(8,128)(2,1)S(1)} %get-tuple-element.8.back, f32[512,1024]{1,0:T(8,128)S(1)} %get-tuple-element.9.base, bf16[512,1024]{1,0:T(8,128)(2,1)S(1)} %get-tuple-element.10.tab), custom_call_target="tpu_custom_call" | custom-call | tf_op jit(solution)/shard_map/image/pallas_call | solution.py:582

commit v5 on v4

--- a/solution.py
+++ b/solution.py
@@ -63,6 +63,21 @@
     return value * jnp.where(lane < value.shape[1] // 2, first, second)
 
 
+def series(square, first, terms):
+    value = jnp.full_like(square, 1.0 / math.factorial(first + 2 * terms))
+    for k in range(terms - 1, -1, -1):
+        value = 1.0 / math.factorial(first + 2 * k) - value * square
+    return value
+
+
+def turns(ticks, whole):
+    turn = ((ticks + whole // 2) & (whole - 1)) - whole // 2
+    angle = turn.astype(F32) * (-math.pi / whole)
+    square = angle * angle
+    sine = angle * series(square, 1, 5)
+    return 1.0 - 2.0 * sine * sine, 2.0 * sine * series(square, 0, 6)
+
+
 def image_rows(blocks):
     half = blocks[0].shape[0] // 2
     cross = []
@@ -79,7 +94,7 @@
     xbuf, obs, cells, counts, turn_in, turn_out, t2, tt, acc, bacc,
     s_send, s_recv, g_send, g_recv, right, right_t, r1r, r1i, left, inner, held,
     r_send, r_recv, b_send, b_recv,
-    tok, in_sem, tab_sem, sa, ra, sb, rb, sc, rc, sd, rd,
+    tok, in_sem, sa, ra, sb, rb, sc, rc, sd, rd,
 ):
     f = lax.axis_index("facet")
     c = lax.axis_index("col")
@@ -88,7 +103,7 @@
     two = 2 * window
     parts = window // 16
     pc = nf
-    rows = xbuf.shape[0] // 2
+    rows = xbuf.shape[1]
     groups = nf // 8
     vis = obs.shape[2]
     if nc % 2:
@@ -162,39 +177,58 @@
 
     far_groups = list(range(n_groups - 1, 0, -1)) if wide == 2 else list(range(1, nc))
 
-    def tab_load(d, lanes, sem):
-        at = pl.ds(pl.multiple_of(group_at(d) * 2 * chunk, 2 * chunk), 2 * chunk)
-        return pltpu.make_async_copy(ctab_hbm.at[at, lanes], tab.at[at, lanes], sem)
-
-    quarter = xbuf.shape[1] // 4
+    extent = xbuf.shape[2]
+    quarter = extent // 4
     depths = [slice(0, quarter), slice(quarter, 2 * quarter), slice(2 * quarter, 4 * quarter)]
-    early = [
-        [tab_load(d, lanes, tab_sem.at[k, d]) for d in far_groups]
-        + [
-            pltpu.make_async_copy(
-                x_hbm.at[p, :, lanes], xbuf.at[p * rows : (p + 1) * rows, lanes], in_sem.at[2 * k + p]
-            )
-            for p in range(2)
-        ]
-        for k, lanes in enumerate(depths)
+    x_loads = [
+        pltpu.make_async_copy(x_hbm.at[:, :, lanes], xbuf.at[:, :, lanes], in_sem.at[n])
+        for n, lanes in enumerate(depths)
     ]
-    mine_load = tab_load(0, slice(None), tab_sem.at[0, 0])
-    row_load = pltpu.make_async_copy(rtab_hbm, t2, in_sem.at[13])
+    mine_at = pl.ds(pl.multiple_of(group_at(0) * 2 * chunk, 2 * chunk), 2 * chunk)
+    mine_load = pltpu.make_async_copy(ctab_hbm.at[mine_at], tab.at[mine_at], in_sem.at[3])
+    row_load = pltpu.make_async_copy(rtab_hbm, t2, in_sem.at[9])
     small_loads = [
-        pltpu.make_async_copy(turn_hbm.at[f, c], turn_in, in_sem.at[8]),
-        pltpu.make_async_copy(turn_hbm.at[:, c, f], turn_out, in_sem.at[9]),
-        pltpu.make_async_copy(obs_hbm, obs, in_sem.at[10]),
-        pltpu.make_async_copy(cells_hbm, cells, in_sem.at[11]),
-        pltpu.make_async_copy(counts_hbm, counts, in_sem.at[12]),
+        pltpu.make_async_copy(turn_hbm.at[f, c], turn_in, in_sem.at[4]),
+        pltpu.make_async_copy(turn_hbm.at[:, c, f], turn_out, in_sem.at[5]),
+        pltpu.make_async_copy(obs_hbm, obs, in_sem.at[6]),
+        pltpu.make_async_copy(cells_hbm, cells, in_sem.at[7]),
+        pltpu.make_async_copy(counts_hbm, counts, in_sem.at[8]),
     ]
-    turned_load = pltpu.make_async_copy(ttab_hbm, tt, in_sem.at[14])
-    for load in sum(early, []):
+    turned_load = pltpu.make_async_copy(ttab_hbm, tt, in_sem.at[10])
+    for load in x_loads:
         load.start()
+
+    spacing = IMAGE // extent
+    lr, li = turns(
+        lax.broadcasted_iota(jnp.int32, (16, extent), 0)
+        * lax.broadcasted_iota(jnp.int32, (16, extent), 1),
+        extent,
+    )
+    high_rows = lax.broadcasted_iota(jnp.int32, (wide * parts, extent), 0)
+    place_q = lax.broadcasted_iota(jnp.int32, (wide * parts, extent), 1)
+    taper = 0.8 - 0.2 * turns(2 * place_q + 1, 2 * extent)[0]
+    taper *= 1.0 / math.sqrt(extent)
+    for d in far_groups:
+        cols = wide * group_at(d) + high_rows // parts
+        freqs = cols * (IMAGE // 4) + ((29 * cols + 3) & (spacing - 1))
+        freqs += spacing * 16 * (high_rows & (parts - 1))
+        hr, hi = turns(freqs * place_q, IMAGE)
+        hr, hi = hr * taper, hi * taper
+        for i in range(wide * parts):
+            er, ei = hr[i : i + 1], hi[i : i + 1]
+            k, u = i // parts, i % parts
+            at = group_at(d) * 2 * chunk + u // 2 * chunk + k * window + u % 2 * 16
+            at = pl.multiple_of(at, 16)
+            tab[pl.ds(at, 16), :] = (lr * er - li * ei).astype(BF)
+            tab[pl.ds(at + half, 16), :] = (lr * ei + li * er).astype(BF)
 
     def strip_term(d, lanes):
         at = pl.multiple_of(group_at(d) * 2 * chunk, 2 * chunk)
         return lax.dot_general(
-            tab[pl.ds(at, 2 * chunk), lanes], xbuf[:, lanes], NT, preferred_element_type=F32
+            tab[pl.ds(at, 2 * chunk), lanes],
+            xbuf[:, :, lanes].reshape(2 * rows, -1),
+            NT,
+            preferred_element_type=F32,
         )
 
     def strips(d, both):
@@ -205,20 +239,22 @@
                 block = [real[:, :rows] - imag[:, rows:], imag[:, :rows] + real[:, rows:]]
                 s_send[wide * group_at(d) + k, part] = jnp.concatenate(block, axis=0).astype(BF)
 
-    def strip_link(step, part):
+    messages = [[0], [1], list(range(2, parts))]
+
+    def strip_link(step, some):
         peer = col_at(step, 1)
-        at = ra.at[part * len(far_steps) + far_steps.index(step)]
-        return col_link(s_send.at[peer, part], s_recv.at[c, part], sa.at[0], at, peer)
+        at = ra.at[messages.index(some) * len(far_steps) + far_steps.index(step)]
+        some = slice(some[0], some[-1] + 1)
+        return col_link(s_send.at[peer, some], s_recv.at[c, some], sa.at[0], at, peer)
 
     def near_link(step):
         peer = col_at(step, 1)
-        at = ra.at[parts * len(far_steps) + near_steps.index(step)]
+        at = ra.at[len(messages) * len(far_steps) + near_steps.index(step)]
         return col_link(s_send.at[peer], s_recv.at[c], sa.at[0], at, peer)
 
     sums = [0.0] * len(far_groups)
-    for lanes, loads in zip(depths, early):
-        for load in loads:
-            load.wait()
+    for lanes, load in zip(depths, x_loads):
+        load.wait()
         if lanes is depths[0]:
             mine_load.start()
             for load in small_loads:
@@ -231,9 +267,9 @@
         strips(d, both)
     greeted = (low, high, place == 1, place == last_place - 1)
     pl.semaphore_wait(barrier, nc + sum(one.astype(jnp.int32) for one in greeted))
-    for part in range(parts):
+    for some in messages:
         for step in far_steps:
-            strip_link(step, part).start()
+            strip_link(step, some).start()
     pl.when((place == 1) & high)(lambda: signal(tok.at[0], f + 2, c))
     pl.when((place == last_place - 1) & low)(lambda: signal(tok.at[1], f - 2, c))
     mine_load.wait()
@@ -271,19 +307,8 @@
     first = cells[0, pl.ds(f, 1), :]
     second = cells[1, pl.ds(f, 1), :]
 
-    def series(square, first, terms):
-        value = jnp.full_like(square, 1.0 / math.factorial(first + 2 * terms))
-        for k in range(terms - 1, -1, -1):
-            value = 1.0 / math.factorial(first + 2 * k) - value * square
-        return value
-
     def wave(count, step, cell):
-        index = step * lax.broadcasted_iota(jnp.int32, (count, vis), 0)
-        turn = ((index * cell + S // 2) & (S - 1)) - S // 2
-        angle = turn.astype(F32) * (-math.pi / S)
-        square = angle * angle
-        sine = angle * series(square, 1, 5)
-        return 1.0 - 2.0 * sine * sine, 2.0 * sine * series(square, 0, 6)
+        return turns(step * lax.broadcasted_iota(jnp.int32, (count, vis), 0) * cell, S)
 
     scale = 1.0 / math.sqrt(vis)
     live = lax.broadcasted_iota(jnp.int32, (1, vis), 1) < counts[f]
@@ -312,8 +337,7 @@
         lo, hi = some[0], some[-1] + 1
         total = acc[lo * half : hi * half]
         for step in far_steps:
-            for part in some:
-                strip_link(step, part).wait_recv()
+            strip_link(step, some).wait_recv()
             src = col_at(step, -1)
             block = s_recv[src, lo:hi].reshape((hi - lo) * half, rows)
             total += window_term(block, src)
@@ -333,10 +357,10 @@
         for part in some:
             send_windows(part)
 
-    windows([0])
-
-    windows([1])
-    windows(list(range(2, parts)))
+    windows(messages[0])
+
+    windows(messages[1])
+    windows(messages[2])
     row_load.start()
 
     l0r, l0i = wave(16, 1, first)
@@ -382,15 +406,11 @@
     for g in range(groups):
         inner[g * two : (g + 1) * two] = pred_term(early_parts, g)
 
-    for part in late_parts[:-1]:
-        take_windows([part])
-        for g in range(groups):
-            inner[g * two : (g + 1) * two] += pred_term([part], g)
-    take_windows(late_parts[-1:])
+    take_windows(late_parts)
     res_r, res_i = obs[0, pl.ds(f, 1), :], obs[1, pl.ds(f, 1), :]
     for g in range(groups):
         at = slice(g * two, (g + 1) * two)
-        value = inner[at] + pred_term(late_parts[-1:], g)
+        value = inner[at] + pred_term(late_parts, g)
         unscale = 1.0 / (scale * S)
         res_r -= jnp.sum(value * left[0, at], axis=0, keepdims=True) * unscale
         res_i -= jnp.sum(value * left[1, at], axis=0, keepdims=True) * unscale
@@ -420,23 +440,26 @@
                     block -= pltpu.roll(u, window, 1) * cross + v * sign(cross, -1.0, 1.0)
                     r_send[part * nf + g * 8 + b] = block.astype(BF)
 
+    def send_backs(part, lo, hi):
+        for index in range(lo, hi):
+            send_back(part, index)
+
     grid_blocks(0, 2)
+    send_backs(0, 0, 2)
+    grid_blocks(2, 5)
+    send_backs(1, 0, 2)
+    grid_blocks(5, 8)
     for part in range(2):
-        for index in range(2):
-            send_back(part, index)
-    grid_blocks(2, 8)
-    for part in range(2):
-        for index in range(2, nf):
-            send_back(part, index)
+        send_backs(part, 2, nf)
         r_recv[part * nf + f] = r_send[part * nf + f]
 
     row_load.wait()
 
-    def back_term(part, pairs):
-        total = None
+    def back_blocks(part, pairs):
         group = waits.index(pairs)
         count = 4 * groups - (0 in pairs)
         sum_of(r_recv, part * nf, count, sc.at[0], rc.at[2 * part + group]).wait_recv()
+        blocks = []
         for q in pairs:
             for g in range(groups):
                 first = g * 8 + 2 * pair_at(q)
@@ -445,33 +468,41 @@
                 block = jnp.concatenate(
                     [jnp.concatenate(pieces, axis=1), jnp.concatenate(spun, axis=1)], axis=0
                 )
-                at = pl.multiple_of(first * two, 2 * two)
-                term = jnp.dot(block, t2[pl.ds(at, 2 * two), :], preferred_element_type=F32)
-                total = term if total is None else total + term
-        return total
+                blocks.append((block, pl.multiple_of(first * two, 2 * two)))
+        return blocks
+
+    def back_term(blocks, lanes):
+        return sum(
+            jnp.dot(block, t2[pl.ds(at, 2 * two), lanes], preferred_element_type=F32)
+            for block, at in blocks
+        )
 
     def back_strips(part):
-        total = (bacc[...] + back_term(part, waits[1])).astype(BF)
-        for cp in range(nc):
-            b_send[part * nc + cp] = total[:, cp * rows : (cp + 1) * rows]
-        for step in col_steps:
-            peer = col_at(step, 1)
-            at = rd.at[0 if step in near_steps else 1 + part]
-            col_link(
-                b_send.at[part * nc + peer], b_recv.at[part * nc + c], sd.at[0], at, peer
-            ).start()
+        blocks = back_blocks(part, waits[1])
+        for d in far_groups + [0]:
+            col = wide * group_at(d)
+            lanes = pl.ds(pl.multiple_of(col * rows, wide * rows), wide * rows)
+            total = (bacc[:, lanes] + back_term(blocks, lanes)).astype(BF)
+            for k in range(wide):
+                b_send[part * nc + col + k] = total[:, k * rows : (k + 1) * rows]
+            for step in col_steps:
+                if step[0] == d:
+                    peer = col_at(step, 1)
+                    at = rd.at[0 if step in near_steps else 1 + part]
+                    col_link(
+                        b_send.at[part * nc + peer], b_recv.at[part * nc + c], sd.at[0], at, peer
+                    ).start()
         b_recv[part * nc + c] = b_send[part * nc + c]
 
-    bacc[...] = back_term(0, waits[0])
+    bacc[...] = back_term(back_blocks(0, waits[0]), slice(None))
     back_strips(0)
-    bacc[...] = back_term(1, waits[0])
+    bacc[...] = back_term(back_blocks(1, waits[0]), slice(None))
     back_strips(1)
     if near_steps:
         sum_of(b_recv, 0, 2 * len(near_steps), sd.at[0], rd.at[0]).wait_recv()
     mine = [b_recv[part * nc + wide * group_at(0) + k] for part in range(2) for k in range(wide)]
-    at = pl.multiple_of(group_at(0) * 2 * chunk, 2 * chunk)
     base_out[...] = jnp.dot(
-        image_rows(mine), tab[pl.ds(at, 2 * chunk), :], preferred_element_type=F32
+        image_rows(mine), tab[mine_at, :], preferred_element_type=F32
     )
     for part in range(2):
         sum_of(b_recv, 0, len(far_steps), sd.at[0], rd.at[1 + part]).wait_recv()
@@ -540,7 +571,7 @@
             in_specs=[hbm] * 8,
             out_specs=(vmem, vmem, vmem),
             scratch_shapes=[
-                pltpu.VMEM((2 * rows, extent), BF),
+                pltpu.VMEM((2, rows, extent), BF),
                 pltpu.VMEM((2, pc, vis), F32),
                 pltpu.VMEM((2, pc, vis), jnp.int32),
                 pltpu.SMEM((pc,), jnp.int32),
@@ -566,8 +597,8 @@
                 pltpu.VMEM((2 * nc, window, rows), BF),
                 pltpu.VMEM((2 * nc, window, rows), BF),
                 pltpu.SemaphoreType.REGULAR((2,)),
-                dma((15,)), dma((4, nc // wide)),
-                dma((1,)), dma((parts * (nc - wide) + wide - 1,)), dma((1,)), dma((parts,)),
+                dma((11,)),
+                dma((1,)), dma((3 * (nc - wide) + wide - 1,)), dma((1,)), dma((parts,)),
                 dma((1,)), dma((4,)), dma((1,)), dma((3,)),
             ],
             compiler_params=pltpu.CompilerParams(

time: 24.6 us -> 24.3 us (0.988)
  no operation moved by 1% of the time
where the time goes in v5:
time: 24.3 us; the launch traced here: 24.2 us
  Pallas kernels  24.2 us (100%)
    pallas_call x1, Pallas kernels, on_device(): pl.pallas_call(functools.partial(cycle_kernel, nf, nc), out_shape=(jax.Sh...  22.5 us
    pallas_call x1, Pallas kernels, on_device(): pl.pallas_call(functools.partial(image_kernel, nc), out_shape=jax.ShapeDt...  1.7 us

profile of v5, /device:TPU:0, one launch (start us, length us, event | category | flops | bytes accessed | tf_op | source)
XLA Modules:
  0.0 24.2 jit_solution(11453534029493869196)
XLA Ops:
  0.0 22.5 %cycle.1 = (bf16[4,64,256]{2,1,0:T(8,128)(2,1)S(1)}, f32[512,1024]{1,0:T(8,128)S(1)}, bf16[512,1024]{1,0:T(8,128)(2,1)S(1)}) custom-call(bf16[2,256,1024]{2,1,0:T(8,128)(2,1)} %x_hbm.1, f32[2,8,1024]{2,1,0:T(8,128)} %obs_hbm.1, s32[2,8,1024]{2,1,0:T(8,128)} %cells_hbm.1, s32[8]{0:T(128)} %counts_hbm.1, bf16[512,1024]{1,0:T(8,128)(2,1)} %constant.8.clone.ctab_hbm, ...), custom_call_target="tpu_custom_call" | custom-call | tf_op jit(solution)/shard_map/cycle/pallas_call | solution.py:564
  22.5 1.7 %image.1 = f32[2,256,1024]{2,1,0:T(8,128)} custom-call(bf16[4,64,256]{2,1,0:T(8,128)(2,1)S(1)} %get-tuple-element.8.back, f32[512,1024]{1,0:T(8,128)S(1)} %get-tuple-element.9.base, bf16[512,1024]{1,0:T(8,128)(2,1)S(1)} %get-tuple-element.10.tab), custom_call_target="tpu_custom_call" | custom-call | tf_op jit(solution)/shard_map/image/pallas_call | solution.py:613

commit v6 on v5

--- a/solution.py
+++ b/solution.py
@@ -296,13 +296,15 @@
     for load in small_loads:
         load.wait()
 
-    def send_windows(part):
+    def send_windows(some):
         def act(index):
-            facet_link(g_send, g_recv, sb.at[0], rb.at[part], part, index).start()
+            for part in some:
+                facet_link(g_send, g_recv, sb.at[0], rb.at[part], part, index).start()
 
         for index in range(nf - 1, -1, -1):
             pl.when(index != f)(functools.partial(act, index))
-        g_recv[part * nf + f] = g_send[part * nf + f]
+        for part in some:
+            g_recv[part * nf + f] = g_send[part * nf + f]
 
     first = cells[0, pl.ds(f, 1), :]
     second = cells[1, pl.ds(f, 1), :]
@@ -354,8 +356,7 @@
         if 0 in some:
             pl.when(far_high & ~low)(lambda: pl.semaphore_wait(tok.at[1], 1))
             pl.when(far_low & ~high)(lambda: pl.semaphore_wait(tok.at[0], 1))
-        for part in some:
-            send_windows(part)
+        send_windows(some)
 
     windows(messages[0])
 
@@ -441,24 +442,29 @@
                     r_send[part * nf + g * 8 + b] = block.astype(BF)
 
     def send_backs(part, lo, hi):
-        for index in range(lo, hi):
-            send_back(part, index)
+        for g in range(groups):
+            for b in range(lo, hi):
+                send_back(part, g * 8 + b)
 
     grid_blocks(0, 2)
     send_backs(0, 0, 2)
+    grid_blocks(5, 8)
+    send_backs(1, 0, 2)
+    for part in range(2):
+        send_backs(part, 5, 8)
     grid_blocks(2, 5)
-    send_backs(1, 0, 2)
-    grid_blocks(5, 8)
     for part in range(2):
-        send_backs(part, 2, nf)
+        send_backs(part, 2, 5)
         r_recv[part * nf + f] = r_send[part * nf + f]
 
     row_load.wait()
 
+    def take_backs(part, pairs):
+        count = 4 * groups - (0 in pairs)
+        at = rc.at[2 * part + waits.index(pairs)]
+        sum_of(r_recv, part * nf, count, sc.at[0], at).wait_recv()
+
     def back_blocks(part, pairs):
-        group = waits.index(pairs)
-        count = 4 * groups - (0 in pairs)
-        sum_of(r_recv, part * nf, count, sc.at[0], rc.at[2 * part + group]).wait_recv()
         blocks = []
         for q in pairs:
             for g in range(groups):
@@ -471,33 +477,48 @@
                 blocks.append((block, pl.multiple_of(first * two, 2 * two)))
         return blocks
 
-    def back_term(blocks, lanes):
+    def lanes_of(d):
+        return pl.ds(pl.multiple_of(wide * group_at(d) * rows, wide * rows), wide * rows)
+
+    def back_term(blocks, d):
         return sum(
-            jnp.dot(block, t2[pl.ds(at, 2 * two), lanes], preferred_element_type=F32)
+            jnp.dot(block, t2[pl.ds(at, 2 * two), lanes_of(d)], preferred_element_type=F32)
             for block, at in blocks
         )
 
-    def back_strips(part):
-        blocks = back_blocks(part, waits[1])
-        for d in far_groups + [0]:
-            col = wide * group_at(d)
-            lanes = pl.ds(pl.multiple_of(col * rows, wide * rows), wide * rows)
-            total = (bacc[:, lanes] + back_term(blocks, lanes)).astype(BF)
-            for k in range(wide):
-                b_send[part * nc + col + k] = total[:, k * rows : (k + 1) * rows]
-            for step in col_steps:
-                if step[0] == d:
-                    peer = col_at(step, 1)
-                    at = rd.at[0 if step in near_steps else 1 + part]
-                    col_link(
-                        b_send.at[part * nc + peer], b_recv.at[part * nc + c], sd.at[0], at, peer
-                    ).start()
+    def keep(part, d, total):
+        for k in range(wide):
+            piece = total[:, k * rows : (k + 1) * rows]
+            b_send[part * nc + wide * group_at(d) + k] = piece.astype(BF)
+
+    def send_strips_back(part, d):
+        for step in col_steps:
+            if step[0] == d:
+                peer = col_at(step, 1)
+                at = rd.at[0 if step in near_steps else 1 + part]
+                col_link(
+                    b_send.at[part * nc + peer], b_recv.at[part * nc + c], sd.at[0], at, peer
+                ).start()
+
+    take_backs(0, waits[0])
+    for d in far_groups:
+        bacc[:, lanes_of(d)] = back_term(back_blocks(0, waits[0]), d)
+    take_backs(0, waits[1])
+    for d in far_groups:
+        keep(0, d, bacc[:, lanes_of(d)] + back_term(back_blocks(0, waits[1]), d))
+        send_strips_back(0, d)
+    for pairs in waits:
+        take_backs(1, pairs)
+    for d in far_groups:
+        keep(1, d, back_term(back_blocks(1, waits[0] + waits[1]), d))
+        send_strips_back(1, d)
+    both = [back_blocks(part, waits[0] + waits[1]) for part in range(2)]
+    both = [(jnp.concatenate([one[0], two_[0]], axis=0), one[1]) for one, two_ in zip(*both)]
+    total = back_term(both, 0)
+    for part in range(2):
+        keep(part, 0, total[part * window : (part + 1) * window])
+        send_strips_back(part, 0)
         b_recv[part * nc + c] = b_send[part * nc + c]
-
-    bacc[...] = back_term(back_blocks(0, waits[0]), slice(None))
-    back_strips(0)
-    bacc[...] = back_term(back_blocks(1, waits[0]), slice(None))
-    back_strips(1)
     if near_steps:
         sum_of(b_recv, 0, 2 * len(near_steps), sd.at[0], rd.at[0]).wait_recv()
     mine = [b_recv[part * nc + wide * group_at(0) + k] for part in range(2) for k in range(wide)]

time: 24.3 us -> 24 us (0.988)
  Pallas kernels: 24.2 us -> 23.9 us
    pallas_call x1, Pallas kernels: 22.5 us -> 22.2 us  [on_device(): pl.pallas_call(functools.partial(cycle_kernel, nf, nc), out_shape=(jax.Sh...]
where the time goes in v6:
time: 24 us; the launch traced here: 23.9 us
  Pallas kernels  23.9 us (100%)
    pallas_call x1, Pallas kernels, on_device(): pl.pallas_call(functools.partial(cycle_kernel, nf, nc), out_shape=(jax.Sh...  22.2 us
    pallas_call x1, Pallas kernels, on_device(): pl.pallas_call(functools.partial(image_kernel, nc), out_shape=jax.ShapeDt...  1.7 us

profile of v6, /device:TPU:0, one launch (start us, length us, event | category | flops | bytes accessed | tf_op | source)
XLA Modules:
  0.0 23.9 jit_solution(1741424022810265146)
XLA Ops:
  0.0 22.2 %cycle.1 = (bf16[4,64,256]{2,1,0:T(8,128)(2,1)S(1)}, f32[512,1024]{1,0:T(8,128)S(1)}, bf16[512,1024]{1,0:T(8,128)(2,1)S(1)}) custom-call(bf16[2,256,1024]{2,1,0:T(8,128)(2,1)} %x_hbm.1, f32[2,8,1024]{2,1,0:T(8,128)} %obs_hbm.1, s32[2,8,1024]{2,1,0:T(8,128)} %cells_hbm.1, s32[8]{0:T(128)} %counts_hbm.1, bf16[512,1024]{1,0:T(8,128)(2,1)} %constant.8.clone.ctab_hbm, ...), custom_call_target="tpu_custom_call" | custom-call | tf_op jit(solution)/shard_map/cycle/pallas_call | solution.py:585
  22.2 1.7 %image.1 = f32[2,256,1024]{2,1,0:T(8,128)} custom-call(bf16[4,64,256]{2,1,0:T(8,128)(2,1)S(1)} %get-tuple-element.8.back, f32[512,1024]{1,0:T(8,128)S(1)} %get-tuple-element.9.base, bf16[512,1024]{1,0:T(8,128)(2,1)S(1)} %get-tuple-element.10.tab), custom_call_target="tpu_custom_call" | custom-call | tf_op jit(solution)/shard_map/image/pallas_call | solution.py:634

commit v7 on v6

--- a/solution.py
+++ b/solution.py
@@ -426,28 +426,31 @@
         pl.when((near < 2) & (index != f))(lambda: act(0))
         pl.when(near >= 2)(lambda: act(1))
 
-    def grid_blocks(lo, hi):
+    def grid_blocks(lo, hi, after=None):
         grid = jnp.dot(held[...], right_t[:, lo * two : hi * two], preferred_element_type=F32)
-        for g in range(groups):
-            block_t = grid[g * two : (g + 1) * two].T
-            for b in range(lo, hi):
-                turn = turn_out[g * 8 + b]
-                same, cross = turn[0:1], turn[1:2]
-                for part in range(2):
+        turned = [grid[g * two : (g + 1) * two].T for g in range(groups)]
+        for part in range(2):
+            for g in range(groups):
+                for b in range(lo, hi):
+                    turn = turn_out[g * 8 + b]
+                    same, cross = turn[0:1], turn[1:2]
                     starts = [(b - lo) * two + (2 * part + k) * half for k in range(2)]
-                    u = jnp.concatenate([block_t[at : at + 16] for at in starts], axis=0)
-                    v = jnp.concatenate([block_t[at + 16 : at + half] for at in starts], axis=0)
+                    u, v = (
+                        jnp.concatenate([turned[g][at + k : at + k + 16] for at in starts], axis=0)
+                        for k in (0, 16)
+                    )
                     block = (u + spin(v, 1.0, -1.0)) * same
                     block -= pltpu.roll(u, window, 1) * cross + v * sign(cross, -1.0, 1.0)
                     r_send[part * nf + g * 8 + b] = block.astype(BF)
+            if after is not None and part == 0:
+                after()
 
     def send_backs(part, lo, hi):
         for g in range(groups):
             for b in range(lo, hi):
                 send_back(part, g * 8 + b)
 
-    grid_blocks(0, 2)
-    send_backs(0, 0, 2)
+    grid_blocks(0, 2, lambda: send_backs(0, 0, 2))
     grid_blocks(5, 8)
     send_backs(1, 0, 2)
     for part in range(2):

time: 24 us -> 24 us (level)
  no operation moved by 1% of the time
where the time goes in v7:
time: 24 us; the launch traced here: 23.9 us
  Pallas kernels  23.9 us (100%)
    pallas_call x1, Pallas kernels, on_device(): pl.pallas_call(functools.partial(cycle_kernel, nf, nc), out_shape=(jax.Sh...  22.2 us
    pallas_call x1, Pallas kernels, on_device(): pl.pallas_call(functools.partial(image_kernel, nc), out_shape=jax.ShapeDt...  1.7 us

profile of v7, /device:TPU:0, one launch (start us, length us, event | category | flops | bytes accessed | tf_op | source)
XLA Modules:
  0.0 23.9 jit_solution(14472700244187060445)
XLA Ops:
  0.0 22.2 %cycle.1 = (bf16[4,64,256]{2,1,0:T(8,128)(2,1)S(1)}, f32[512,1024]{1,0:T(8,128)S(1)}, bf16[512,1024]{1,0:T(8,128)(2,1)S(1)}) custom-call(bf16[2,256,1024]{2,1,0:T(8,128)(2,1)} %x_hbm.1, f32[2,8,1024]{2,1,0:T(8,128)} %obs_hbm.1, s32[2,8,1024]{2,1,0:T(8,128)} %cells_hbm.1, s32[8]{0:T(128)} %counts_hbm.1, bf16[512,1024]{1,0:T(8,128)(2,1)} %constant.8.clone.ctab_hbm, ...), custom_call_target="tpu_custom_call" | custom-call | tf_op jit(solution)/shard_map/cycle/pallas_call | solution.py:588
  22.2 1.7 %image.1 = f32[2,256,1024]{2,1,0:T(8,128)} custom-call(bf16[4,64,256]{2,1,0:T(8,128)(2,1)S(1)} %get-tuple-element.8.back, f32[512,1024]{1,0:T(8,128)S(1)} %get-tuple-element.9.base, bf16[512,1024]{1,0:T(8,128)(2,1)S(1)} %get-tuple-element.10.tab), custom_call_target="tpu_custom_call" | custom-call | tf_op jit(solution)/shard_map/image/pallas_call | solution.py:637

commit v8 on v7

--- a/solution.py
+++ b/solution.py
@@ -451,13 +451,13 @@
                 send_back(part, g * 8 + b)
 
     grid_blocks(0, 2, lambda: send_backs(0, 0, 2))
-    grid_blocks(5, 8)
+    grid_blocks(6, 8)
     send_backs(1, 0, 2)
     for part in range(2):
-        send_backs(part, 5, 8)
-    grid_blocks(2, 5)
+        send_backs(part, 6, 8)
+    grid_blocks(2, 6)
     for part in range(2):
-        send_backs(part, 2, 5)
+        send_backs(part, 2, 6)
         r_recv[part * nf + f] = r_send[part * nf + f]
 
     row_load.wait()

time: 24 us -> 24 us (level)
  no operation moved by 1% of the time
where the time goes in v8:
time: 24 us; the launch traced here: 23.9 us
  Pallas kernels  23.9 us (100%)
    pallas_call x1, Pallas kernels, on_device(): pl.pallas_call(functools.partial(cycle_kernel, nf, nc), out_shape=(jax.Sh...  22.2 us
    pallas_call x1, Pallas kernels, on_device(): pl.pallas_call(functools.partial(image_kernel, nc), out_shape=jax.ShapeDt...  1.7 us

profile of v8, /device:TPU:0, one launch (start us, length us, event | category | flops | bytes accessed | tf_op | source)
XLA Modules:
  0.0 23.9 jit_solution(3328531097167416599)
XLA Ops:
  0.0 22.2 %cycle.1 = (bf16[4,64,256]{2,1,0:T(8,128)(2,1)S(1)}, f32[512,1024]{1,0:T(8,128)S(1)}, bf16[512,1024]{1,0:T(8,128)(2,1)S(1)}) custom-call(bf16[2,256,1024]{2,1,0:T(8,128)(2,1)} %x_hbm.1, f32[2,8,1024]{2,1,0:T(8,128)} %obs_hbm.1, s32[2,8,1024]{2,1,0:T(8,128)} %cells_hbm.1, s32[8]{0:T(128)} %counts_hbm.1, bf16[512,1024]{1,0:T(8,128)(2,1)} %constant.8.clone.ctab_hbm, ...), custom_call_target="tpu_custom_call" | custom-call | tf_op jit(solution)/shard_map/cycle/pallas_call | solution.py:588
  22.2 1.7 %image.1 = f32[2,256,1024]{2,1,0:T(8,128)} custom-call(bf16[4,64,256]{2,1,0:T(8,128)(2,1)S(1)} %get-tuple-element.8.back, f32[512,1024]{1,0:T(8,128)S(1)} %get-tuple-element.9.base, bf16[512,1024]{1,0:T(8,128)(2,1)S(1)} %get-tuple-element.10.tab), custom_call_target="tpu_custom_call" | custom-call | tf_op jit(solution)/shard_map/image/pallas_call | solution.py:637
